TPU v7x, 256 devices: a whole 4x4x8 slice. The times are simulated.
256 devices in a mesh: shard: 64 (over z, y, core), model: 4 (over x).
Axes of the slice: x: 4, y: 4, z: 8, core: 2. Of those that a mesh axis runs over, the one named last changes fastest.
Arguments:
- one_gate: float32 [2048, 8192], P('shard', 'model'), may hold values from -0.375 to 0.375
- other_gate: float32 [2048, 8192], P('shard', 'model'), may hold values from -0.125 to 0.125
- one_up: float32 [2048, 8192], P('shard', 'model'), may hold values from -0.375 to 0.375
- other_up: float32 [2048, 8192], P('shard', 'model'), may hold values from -0.125 to 0.125
- mix_share: float32 [2048], P('shard'), may hold values from 0.2 to 0.8
- norm_train: float32 [2048], P(('shard', 'model')), may hold values from 0.25 to 1.75
- norm_step: float32 [2048], P(('shard', 'model')), may hold values from -0.3 to 0.3
Outputs:
- final_gate: bfloat16 [2048, 8192], P(None, 'model')
- final_up: bfloat16 [2048, 8192], P(None, 'model')
- column_gate: float32 [8192], P('model')
- column_up: float32 [8192], P('model')
- serve_norm: bfloat16 [2048], replicated
All inputs are finite; a program needn't handle non-finite values. Where the computation divides by a largest or mean magnitude, that divisor is 1e-20 or more.
Results may differ from a plain program's by a relative error of at most 0.001.
Values may be sent and summed in bfloat16 or wider, within the bound.
A program may use at most 128 MiB of HBM per device.

v0:
```python
import jax
import jax.numpy as jnp
from jax import lax
from jax.sharding import Mesh
from jax.sharding import PartitionSpec as P

SHARD = ("shard_0", "shard_1", "shard_2")
SHARD_MODEL = ("shard_0", "shard_1", "shard_2", "model")


def copy_for_each(array, axis):
    copies = jnp.broadcast_to(array, (lax.axis_size(axis), *array.shape))
    return lax.all_to_all(copies, axis, split_axis=0, concat_axis=0, tiled=True)


def over_copies(array, axis):
    return copy_for_each(array, axis).max(axis=0)


def in_one(arrays, axis):
    flat, at, outs = (jnp.concatenate([a.reshape(-1) for a in arrays]), 0, [])
    total = over_copies(flat, axis)
    for a in arrays:
        outs.append(total[at : at + a.size].reshape(a.shape))
        at += a.size
    return tuple(outs)


def side_by_side(arrays, axis, dim, along):
    both = jnp.concatenate(arrays, axis=along)
    whole, at, outs = (lax.all_gather(both, axis, axis=dim, tiled=True), 0, [])
    for a in arrays:
        outs.append(lax.slice_in_dim(whole, at, at + a.shape[along], axis=along))
        at += a.shape[along]
    return tuple(outs)


def joined_along(tiles, dim):
    dims = list(tiles.shape[1:])
    dims[dim] *= tiles.shape[0]
    return jnp.moveaxis(tiles, 0, dim).reshape(dims)


def gather_in_order(array, axes, turns):
    tiles = array[None]
    for k in turns:
        tiles = lax.all_gather(tiles, axes[k], axis=0, tiled=True)
    carried = [lax.axis_size(axes[k]) for k in reversed(turns)]
    tiles = tiles.reshape(*carried, *array.shape)
    turned = sorted(range(len(turns)), key=lambda place: turns[len(turns) - 1 - place])
    return tiles.transpose(*turned, *range(len(turns), tiles.ndim)).reshape(-1, *array.shape)


def gathered_by_axis(array, axes, turns, dim):
    return joined_along(gather_in_order(array, axes, turns), dim)


def local(one_gate, other_gate, one_up, other_up, mix_share, norm_train, norm_step):
    result_gate = mix_share[:, None] * one_gate + (1.0 - mix_share[:, None]) * other_gate
    result_up = mix_share[:, None] * one_up + (1.0 - mix_share[:, None]) * other_up
    column_gate, column_up = in_one(
        (jnp.max(jnp.abs(result_gate), axis=0), jnp.max(jnp.abs(result_up), axis=0)), SHARD
    )
    narrow_gate, narrow_up = (
        (result_gate / column_gate).astype(jnp.bfloat16),
        (result_up / column_up).astype(jnp.bfloat16),
    )
    final_gate, final_up = side_by_side((narrow_gate, narrow_up), SHARD, 0, 1)
    serve_norm = gathered_by_axis(
        (norm_train + norm_step).astype(jnp.bfloat16), SHARD_MODEL, (0, 1, 3, 2), 0
    )
    return (final_gate, final_up, column_gate, column_up, serve_norm)


def solution(mesh):
    torus = Mesh(
        mesh.devices.reshape(8, 4, 2, mesh.shape["model"]),
        ("shard_0", "shard_1", "shard_2", "model"),
    )
    return jax.shard_map(
        local,
        mesh=torus,
        in_specs=(
            P(SHARD, "model"),
            P(SHARD, "model"),
            P(SHARD, "model"),
            P(SHARD, "model"),
            P(SHARD),
            P(SHARD_MODEL),
            P(SHARD_MODEL),
        ),
        out_specs=(P(None, "model"), P(None, "model"), P("model"), P("model"), P()),
        check_vma=False,
    )
```

profile of v0, /device:TPU:1, one launch (start us, length us, event | category | flops | bytes accessed | tf_op | source)
XLA Modules:
  0.0 169.9 jit_solution(2794008969568539526)
XLA Ops:
  7.2 0.0 all-gather.4.cloned.1.call-start
  7.2 0.7 broadcast_subtract_fusion
  7.9 1.4 abs_reduce_fusion.1
  9.3 1.0 broadcast_in_dim.4
  10.3 41.1 %all_to_all.6 = f32[64,1,4096]{2,1,0:T(1,128)S(1)} all-to-all(f32[64,1,4096]{2,1,0:T(1,128)S(1)} %broadcast_in_dim.4), channel_id=1, replica_groups=mesh['shard_0'=8,'shard_1'=4,'shard_2'=2,'model'=4] {'shard_0','shard_1'..., dimensions={0} | all-to-all | bytes 2097152 | tf_op jit(solution)/shard_map/all_to_all | solution.py:13
  51.4 0.9 reduce_max.29
  52.3 0.0 copy-start
  52.3 0.0 copy-start.1
  52.3 1.4 divide_convert_fusion.1
  53.6 0.7 pad_maximum_fusion
  54.4 0.0 all-gather.4.cloned.1.call-update
  54.4 1.3 dynamic-slice
  56.3 0.7 add_convert_fusion
  57.0 0.2 dynamic-update-slice
  57.2 12.8 %all-reduce = bf16[64]{0:T(256)(128)(2,1)S(1)} all-reduce(bf16[64]{0:T(256)(128)(2,1)S(1)} %dynamic-update-slice), channel_id=2, replica_groups=mesh['shard_0'=8,'shard_1'=4,'shard_2'=2,'model'=4] {'shard_0'}, use_global_device_ids=true, to_apply=%add | all-reduce | flops 64 | bytes 256
  70.0 0.1 reshape.23
  70.1 8.9 %all_gather.17 = bf16[32,8]{1,0:T(8,128)(2,1)S(1)} all-gather(bf16[8,8]{1,0:T(8,128)(2,1)S(1)} %reshape.23), channel_id=1, replica_groups=mesh['shard_0'=8,'shard_1'=4,'shard_2'=2,'model'=4] {'shard_1'}, dimensions={0}, use_global_device_ids=true | all-gather | bytes 640 | tf_op jit(solution)/shard_map/all_gather | solution.py:47
  79.0 0.1 copy.23
  79.1 8.9 %all-gather.1 = bf16[4,32,8]{1,2,0:T(8,128)(2,1)S(1)} all-gather(bf16[1,32,8]{1,2,0:T(8,128)(2,1)S(1)} %copy.23), channel_id=1, replica_groups=mesh['shard_0'=8,'shard_1'=4,'shard_2'=2,'model'=4] {'model'}, dimensions={0}, use_global_device_ids=true | all-gather | bytes 2560 | tf_op jit(solution)/shard_map/all_gather | solution.py:47
  88.0 0.1 reshape.28
  88.1 9.0 %all_gather.19 = bf16[256,8]{0,1:T(8,128)(2,1)S(1)} all-gather(bf16[128,8]{0,1:T(8,128)(2,1)S(1)} %reshape.28), channel_id=1, replica_groups=mesh['shard_0'=8,'shard_1'=4,'shard_2'=2,'model'=4] {'shard_2'}, dimensions={0}, use_global_device_ids=true | all-gather | bytes 6144 | tf_op jit(solution)/shard_map/all_gather | solution.py:47
  97.1 0.1 reshape.22
  97.3 0.2 copy.25
  97.5 0.7 reshape_reshape.3
  98.2 53.0 %all-gather.4.cloned.1.call-done = bf16[2048,4096]{1,0:T(8,128)(2,1)} async-done(((bf16[32,4096]{1,0:T(8,128)(2,1)}), bf16[2048,4096]{1,0:T(8,128)(2,1)}) %all-gather.4.cloned.1.call-update) | async-done | bytes 16777232 | tf_op jit(solution)/shard_map/all_gather | solution.py:31
  151.1 11.9 %fusion = (bf16[2048,2048]{1,0:T(8,128)(2,1)}, bf16[2048,2048]{1,0:T(8,128)(2,1)}) fusion(bf16[2048,4096]{1,0:T(8,128)(2,1)} %all-gather.4.cloned.1.call-done), kind=kLoop, calls=%fused_computation.10 | loop fusion | bytes 33554432 | tf_op jit(solution)/shard_map/slice | solution.py:33
  163.1 0.0 copy-done
  163.1 0.0 copy-done.1
  (4 shorter events, 0.0 us)
Async XLA Ops:
  7.2 144.0 %all-gather.4.cloned.1.call-start = ((), (), s32[]{:S(2)}) async-start(), calls=%async_computation.1 | async-start | bytes 17039360 | tf_op jit(solution)/shard_map/all_gather | solution.py:31
  52.3 110.8 %copy-start = (f32[2048]{0:T(1024)}, f32[2048]{0:T(1024)S(1)}, u32[]{:S(2)}) copy-start(f32[2048]{0:T(1024)S(1)} %get-tuple-element.9) | copy-start | bytes 24580
  52.3 110.8 %copy-start.1 = (f32[2048]{0:T(1024)}, f32[2048]{0:T(1024)S(1)}, u32[]{:S(2)}) copy-start(f32[2048]{0:T(1024)S(1)} %get-tuple-element.10) | copy-start | bytes 24580
Sparse Core Ops, SparseCore 0:
  54.5 96.5 all-gather.3
where the time goes:
time: 170 us
  blocking collectives  80.8 us (48%)
  waiting for transfers between devices  53 us (31%)
  local copies, waits for them, and re-layouts  15.7 us (9%)
  between operations  14.8 us (9%)
  other arithmetic  5.66 us (3%)
    all_gather x1, waiting for transfers between devices, side_by_side(): whole, at, outs = (lax.all_gather(both, axis, axis=dim, tiled=True), 0, [])  53 us
    all_to_all x1, blocking collectives, copy_for_each(): return lax.all_to_all(copies, axis, split_axis=0, concat_axis=0, tiled=True)  41.1 us
    all_gather x3, blocking collectives, gather_in_order(): tiles = lax.all_gather(tiles, axes[k], axis=0, tiled=True)  26.8 us
    unnamed x1, blocking collectives  12.8 us
    slice x1, local copies, waits for them, and re-layouts, side_by_side(): outs.append(lax.slice_in_dim(whole, at, at + a.shape[along], axis=along))  11.9 us
  transfers between devices with their start and end apart: 1, of which 1 were waited for; matrix products, arithmetic and copies ran while one was open for 2% of the time, Pallas kernels for 0%

commit v1 on v0

v1 whole, which is shorter than its diff:
```python
import heapq

import jax
import jax.numpy as jnp
from jax import lax
from jax.experimental import pallas as pl
from jax.experimental.pallas import tpu as pltpu
from jax.sharding import Mesh
from jax.sharding import PartitionSpec as P

SHARD = ("shard_0", "shard_1", "shard_2")
SHARD_MODEL = ("shard_0", "shard_1", "shard_2", "model")

Z, Y, C, X = 8, 4, 2, 4
ROWS, COLS, OWN = 2048, 2048, 32
CHIP = C * OWN
TILES = COLS // 128
LOW = -3.0e38

PIECES = (("B", 0, 6, 11), ("B", 1, 11, 16), ("A", 0, 0, 3), ("A", 1, 3, 6))


def reach(half, n):
    return (n // 2, n // 2 - 1) if half == 0 else (n // 2 - 1, n // 2)


def forwards(piece, dz, dy):
    kind, half = PIECES[piece][:2]
    zp, zm = reach(half, Z)
    yp, ym = reach(half, Y)
    along_z, along_y = [], []
    if 0 <= dz < zp:
        along_z.append(("z+", dz + 1, dy))
    if -zm < dz <= 0:
        along_z.append(("z-", dz - 1, dy))
    if 0 <= dy < yp:
        along_y.append(("y+", dz, dy + 1))
    if -ym < dy <= 0:
        along_y.append(("y-", dz, dy - 1))
    if kind == "A":
        return along_z + (along_y if dz == 0 else [])
    return (along_z if dy == 0 else []) + along_y


def arrivals(hop=2.0, turn=0.05, rate=1.0 / 5.6):
    free = dict.fromkeys(("y+", "y-", "z+", "z-"), 0.0)
    queue, count, clock, order = [], 0, 0.0, []

    def issue(piece, dz, dy, at):
        nonlocal count
        for link, z, y in forwards(piece, dz, dy):
            width = (PIECES[piece][3] - PIECES[piece][2]) / TILES
            free[link] = max(at, free[link]) + width / rate
            count += 1
            heapq.heappush(queue, (free[link] + hop, count, piece, z, y))

    for piece in range(len(PIECES)):
        issue(piece, 0, 0, clock)
        clock += 2 * turn
    while queue:
        at, _, piece, dz, dy = heapq.heappop(queue)
        clock = max(clock, at) + turn
        order.append((piece, dz, dy))
        issue(piece, dz, dy, clock)
        clock += turn
    return order


def gather_kernel(
    mix_h, one_g, other_g, one_u, other_u, train_h, step_h,
    out, cols, norm,
    mix, train, step, ins, theirs, x, peak, peak_y, peak1, peak_z, peak2,
    row0, row_x, row1, row_c, row2, row_y,
    in_sem, x_sem, peak_send, y_sem, z_sem, col_sem, norm_send, norm_sem,
    send_sem, recv_sem, side_send, side_recv,
):
    z, y, c, m = (lax.axis_index(a) for a in ("shard_0", "shard_1", "shard_2", "model"))

    def device(z, y, c, m):
        return (z, y, c, m)

    z_at = [device(lax.rem(z + d, Z), y, c, m) for d in range(Z)]
    y_at = [device(z, lax.rem(y + d, Y), c, m) for d in range(Y)]
    m_at = [device(z, y, c, lax.rem(m + d, X)) for d in range(X)]
    sibling = device(z, y, 1 - c, m)
    link_to = {"z+": z_at[1], "z-": z_at[Z - 1], "y+": y_at[1], "y-": y_at[Y - 1]}

    def remote(src, dst, send, recv, to):
        return pltpu.make_async_remote_copy(
            src_ref=src, dst_ref=dst, send_sem=send, recv_sem=recv,
            device_id=to, device_id_type=pl.DeviceIdType.MESH,
        )

    partners = [sibling, *y_at[1:], *z_at[1:], *m_at[1:]]
    barrier = pltpu.get_barrier_semaphore()
    for to in partners:
        pl.semaphore_signal(barrier, inc=1, device_id=to, device_id_type=pl.DeviceIdType.MESH)

    gate, up = 2 * (1 - c), 2 * c
    small = [
        pltpu.make_async_copy(mix_h, mix, in_sem.at[4]),
        pltpu.make_async_copy(train_h, train, in_sem.at[5]),
        pltpu.make_async_copy(step_h, step, in_sem.at[6]),
    ]
    large = [
        pltpu.make_async_copy(one_g, ins.at[gate], in_sem.at[gate]),
        pltpu.make_async_copy(other_g, ins.at[gate + 1], in_sem.at[gate + 1]),
        pltpu.make_async_copy(one_u, ins.at[up], in_sem.at[up]),
        pltpu.make_async_copy(other_u, ins.at[up + 1], in_sem.at[up + 1]),
    ]
    for copy in small + large:
        copy.start()
    for copy in small:
        copy.wait()

    sub = lax.broadcasted_iota(jnp.int32, (8, 128), 0)
    shares = []
    for r in range(OWN // 8):
        share = jnp.full((8, 128), mix[8 * r], jnp.float32)
        for i in range(1, 8):
            share = jnp.where(sub == i, mix[8 * r + i], share)
        shares.append((share, 1.0 - share))

    def blend(slot, store):
        for k in (slot, slot + 1):
            pltpu.make_async_copy(one_g, ins.at[k], in_sem.at[k]).wait()
        for t in range(TILES):
            lanes = slice(128 * t, 128 * t + 128)
            for r, (share, rest) in enumerate(shares):
                rows = slice(8 * r, 8 * r + 8)
                store(r, lanes, share * ins[slot, rows, lanes] + rest * ins[slot + 1, rows, lanes])

    def store_theirs(r, lanes, value):
        theirs[8 * r : 8 * r + 8, lanes] = value

    def store_own(r, lanes, value):
        x[pl.ds(pl.multiple_of(OWN * c + 8 * r, 8), 8), lanes] = value

    blend(0, store_theirs)

    lane2 = lax.broadcasted_iota(jnp.int32, (2, 128), 1)
    sub2 = lax.broadcasted_iota(jnp.int32, (2, 128), 0)
    start = (lax.rem(y, 2) * C + c) * OWN + m * 8
    line = jnp.full((2, 128), LOW, jnp.float32)
    for i in range(8):
        line = jnp.where((lane2 == start + i) & (sub2 == y // 2), train[i] + step[i], line)
    row0[...] = line

    pl.semaphore_wait(barrier, len(partners))

    to_sibling = remote(
        theirs, x.at[pl.ds(pl.multiple_of(OWN * c, OWN), OWN)], x_sem.at[0], x_sem.at[1], sibling
    )
    to_sibling.start()
    norm_x = [remote(row0, row_x.at[d], norm_send.at[0], norm_sem.at[d], m_at[d]) for d in range(1, X)]
    for copy in norm_x:
        copy.start()
    blend(2, store_own)

    def peak_of(t, first):
        lanes = slice(128 * t, 128 * t + 128)
        best = jnp.abs(x[pl.ds(pl.multiple_of(first, 8), 8), lanes])
        for r in range(1, OWN // 8):
            best = jnp.maximum(best, jnp.abs(x[pl.ds(pl.multiple_of(first + 8 * r, 8), 8), lanes]))
        return best

    own_peaks = [peak_of(t, OWN * c) for t in range(TILES)]
    to_sibling.wait_recv()
    for t in range(TILES):
        best = jnp.maximum(own_peaks[t], peak_of(t, OWN * (1 - c)))
        peak[t : t + 1, :] = jnp.max(best, axis=0, keepdims=True)

    over_y = [remote(peak, peak_y.at[d], peak_send.at[0], y_sem.at[d], y_at[d]) for d in range(1, Y)]
    for copy in over_y:
        copy.start()
    best = peak[...]
    for d, copy in enumerate(over_y, 1):
        copy.wait_recv()
        best = jnp.maximum(best, peak_y[d])
    peak1[...] = best

    over_z = [remote(peak1, peak_z.at[d], peak_send.at[1], z_sem.at[d], z_at[d]) for d in range(1, Z)]
    for copy in over_z:
        copy.start()
    for d, copy in enumerate(over_z, 1):
        copy.wait_recv()
        best = jnp.maximum(best, peak_z[d])
    peak2[...] = best
    cols[c] = best

    def block_at(dz, dy):
        chip = lax.rem(z - dz + Z, Z) * Y + lax.rem(y - dy + Y, Y)
        return pl.multiple_of(chip * CHIP, CHIP)

    home = block_at(0, 0)

    def scale(piece):
        for t in range(*PIECES[piece][2:]):
            lanes = slice(128 * t, 128 * t + 128)
            by = jnp.broadcast_to(peak2[t : t + 1, :], (16, 128))
            for r in range(CHIP // 16):
                rows = pl.ds(pl.multiple_of(home + 16 * r, 16), 16)
                out[c, rows, lanes] = (x[16 * r : 16 * r + 16, lanes] / by).astype(jnp.bfloat16)

    def flag(piece, dz, dy):
        return recv_sem.at[piece, (dz % Z) * Y + dy % Y]

    def part(piece, base):
        first, last = PIECES[piece][2:]
        return out.at[c, pl.ds(base, CHIP), pl.ds(128 * first, 128 * (last - first))]

    def send_on(piece, dz, dy, base):
        ref = part(piece, base)
        for link, to_z, to_y in forwards(piece, dz, dy):
            remote(ref, ref, send_sem.at[0], flag(piece, to_z, to_y), link_to[link]).start()

    def send_aside(base):
        ref = out.at[c, pl.ds(base, CHIP)]
        remote(ref, ref, side_send.at[0], side_recv.at[0], sibling).start()

    scale(0)
    for piece in range(len(PIECES)):
        if piece + 1 < len(PIECES):
            scale(piece + 1)
        send_on(piece, 0, 0, home)
    send_aside(home)
    col_copy = remote(cols.at[c], cols.at[c], col_sem.at[0], col_sem.at[1], sibling)
    col_copy.start()

    n_wait = {}

    def norm_over_x():
        line = row0[...]
        for d, copy in enumerate(norm_x, 1):
            copy.wait_recv()
            line = jnp.maximum(line, row_x[d])
        row1[...] = line
        n_wait["c"] = remote(row1, row_c, norm_send.at[1], norm_sem.at[4], sibling)
        n_wait["c"].start()

    def norm_over_core():
        n_wait["c"].wait_recv()
        row2[...] = jnp.maximum(row1[...], row_c[...])
        n_wait["y"] = [
            remote(row2, row_y.at[d], norm_send.at[2], norm_sem.at[4 + d], y_at[d]) for d in range(1, Y)
        ]
        for copy in n_wait["y"]:
            copy.start()

    def norm_over_y():
        line = row2[...]
        for d, copy in enumerate(n_wait["y"], 1):
            copy.wait_recv()
            line = jnp.maximum(line, row_y[d])
        norm[z] = line
        n_wait["z"] = [
            remote(norm.at[z], norm.at[z], norm_send.at[3], norm_sem.at[7 + d], z_at[d]) for d in range(1, Z)
        ]
        for copy in n_wait["z"]:
            copy.start()

    aside = {12: norm_over_x, 36: norm_over_core, 64: norm_over_y}
    seen = {}
    for k, (piece, dz, dy) in enumerate(arrivals()):
        if k in aside:
            aside[k]()
        base = block_at(dz, dy)
        ref = part(piece, base)
        remote(ref, ref, send_sem.at[0], flag(piece, dz, dy), sibling).wait_recv()
        send_on(piece, dz, dy, base)
        seen[dz % Z, dy % Y] = seen.get((dz % Z, dy % Y), 0) + 1
        if seen[dz % Z, dy % Y] == len(PIECES):
            send_aside(base)

    for copy in n_wait["z"]:
        copy.wait_recv()
    col_copy.wait()
    to_sibling.wait_send()
    for copy in norm_x + [n_wait["c"]] + n_wait["y"] + n_wait["z"] + over_y + over_z:
        copy.wait_send()
    others = out.at[0, pl.ds(0, ROWS - CHIP)]
    pltpu.make_async_copy(others, others, send_sem.at[0]).wait()
    whole = out.at[0]
    pltpu.make_async_copy(whole, whole, side_send.at[0]).wait()
    pltpu.make_async_copy(whole, whole, side_recv.at[0]).wait()


def write_kernel(tiles, cols, norm, gate, up, col_gate, col_up, gain, sem):
    parts = 4
    rows = ROWS // parts
    copies = []
    for i, ref in enumerate((gate, up)):
        for k in range(parts):
            at = pl.ds(k * rows, rows)
            copies.append(pltpu.make_async_copy(tiles.at[i, at], ref.at[at], sem.at[i * parts + k]))
    for copy in copies:
        copy.start()
    col_gate[...] = cols[0]
    col_up[...] = cols[1]
    gain[...] = jnp.concatenate([norm[k] for k in range(Z)], axis=0).astype(jnp.bfloat16)
    for copy in copies:
        copy.wait()


def local(one_gate, other_gate, one_up, other_up, mix_share, norm_train, norm_step):
    f32, bf16 = jnp.float32, jnp.bfloat16
    hbm_spec = pl.BlockSpec(memory_space=pltpu.HBM)
    vmem_spec = pl.BlockSpec(memory_space=pltpu.VMEM)
    dma = pltpu.SemaphoreType.DMA
    tiles, cols, norm = pl.pallas_call(
        gather_kernel,
        out_shape=(
            pltpu.VMEM((2, ROWS, COLS), bf16),
            pltpu.VMEM((2, TILES, 128), f32),
            pltpu.VMEM((Z, 2, 128), f32),
        ),
        in_specs=[hbm_spec] * 7,
        out_specs=(vmem_spec,) * 3,
        scratch_shapes=[
            pltpu.SMEM((OWN,), f32), pltpu.SMEM((8,), f32), pltpu.SMEM((8,), f32),
            pltpu.VMEM((4, OWN, COLS), f32),
            pltpu.VMEM((OWN, COLS), f32),
            pltpu.VMEM((CHIP, COLS), f32),
            pltpu.VMEM((TILES, 128), f32),
            pltpu.VMEM((Y, TILES, 128), f32),
            pltpu.VMEM((TILES, 128), f32),
            pltpu.VMEM((Z, TILES, 128), f32),
            pltpu.VMEM((TILES, 128), f32),
            pltpu.VMEM((2, 128), f32),
            pltpu.VMEM((X, 2, 128), f32),
            pltpu.VMEM((2, 128), f32),
            pltpu.VMEM((2, 128), f32),
            pltpu.VMEM((2, 128), f32),
            pltpu.VMEM((Y, 2, 128), f32),
            dma((7,)), dma((2,)), dma((2,)), dma((Y,)), dma((Z,)), dma((2,)), dma((4,)), dma((7 + Z,)),
            dma((1,)), dma((len(PIECES), Z * Y)), dma((1,)), dma((1,)),
        ],
        compiler_params=pltpu.CompilerParams(
            collective_id=0, has_side_effects=True, vmem_limit_bytes=24 * 2**20
        ),
        name="gather",
    )(
        *(
            pltpu.with_memory_space_constraint(a, pltpu.HBM)
            for a in (mix_share, one_gate, other_gate, one_up, other_up, norm_train, norm_step)
        )
    )
    tiles, cols, norm = (pltpu.with_memory_space_constraint(a, pltpu.VMEM) for a in (tiles, cols, norm))
    gate, up, col_gate, col_up, gain = pl.pallas_call(
        write_kernel,
        out_shape=(
            jax.ShapeDtypeStruct((ROWS, COLS), bf16),
            jax.ShapeDtypeStruct((ROWS, COLS), bf16),
            jax.ShapeDtypeStruct((TILES, 128), f32),
            jax.ShapeDtypeStruct((TILES, 128), f32),
            jax.ShapeDtypeStruct((2 * Z, 128), bf16),
        ),
        in_specs=[vmem_spec] * 3,
        out_specs=(hbm_spec, hbm_spec, vmem_spec, vmem_spec, vmem_spec),
        scratch_shapes=[dma((8,))],
        compiler_params=pltpu.CompilerParams(vmem_limit_bytes=8 * 2**20),
        name="write",
    )(tiles, cols, norm)
    return gate, up, col_gate.reshape(COLS), col_up.reshape(COLS), gain.reshape(ROWS)


def solution(mesh):
    torus = Mesh(mesh.devices.reshape(Z, Y, C, X), SHARD_MODEL)
    return jax.shard_map(
        local,
        mesh=torus,
        in_specs=(
            P(SHARD, "model"), P(SHARD, "model"), P(SHARD, "model"), P(SHARD, "model"),
            P(SHARD), P(SHARD_MODEL), P(SHARD_MODEL),
        ),
        out_specs=(P(None, "model"), P(None, "model"), P("model"), P("model"), P()),
        check_vma=False,
    )
```

time: 170 us -> 75.8 us (0.45)
  blocking collectives: 80.8 us -> 0 us
  Pallas kernels: 0 us -> 75 us
  waiting for transfers between devices: 53 us -> 0 us
  local copies, waits for them, and re-layouts: 15.7 us -> 0 us
  between operations: 14.8 us -> 0.64 us
  other arithmetic: 5.66 us -> 0 us
    pallas_call x0 -> x2, Pallas kernels: none -> 75 us  [the longest x1 68.5 us: local(): pl.pallas_call(gather_kernel, out_shape=(pltpu.VMEM((2, ROWS, COLS), bf16...]
    all_gather x1 -> x0, waiting for transfers between devices: 53 us -> none  [side_by_side(): whole, at, outs = (lax.all_gather(both, axis, axis=dim, tiled=True), 0, [])]
    all_to_all x1 -> x0, blocking collectives: 41.1 us -> none  [copy_for_each(): return lax.all_to_all(copies, axis, split_axis=0, concat_axis=0, tiled=True)]
    all_gather x3 -> x0, blocking collectives: 26.8 us -> none  [gather_in_order(): tiles = lax.all_gather(tiles, axes[k], axis=0, tiled=True)]
    unnamed x1 -> x0, blocking collectives: 12.8 us -> none
    slice x2 -> x0, local copies, waits for them, and re-layouts: 12 us -> none  [the longest x1 11.9 us: side_by_side(): outs.append(lax.slice_in_dim(whole, at, at + a.shape[along], axis=along))]
    reduce_max x2 -> x0, other arithmetic: 2.24 us -> none  [the longest x1 1.38 us: local(): jnp.max(jnp.abs(result_gate), axis=0)]
    convert_element_type x2 -> x0, other arithmetic: 2.04 us -> none  [the longest x1 1.36 us: local(): (result_gate / column_gate).astype(jnp.bfloat16)]
  transfers between devices with their start and end apart: 1 -> 0, of which waited for: 1 -> 0; matrix products, arithmetic and copies ran while one was open for 2% -> 0% of each run, Pallas kernels for 0% -> 0%
where the time goes in v1:
time: 75.8 us; the launch traced here: 75.7 us
  Pallas kernels  75 us (99%)
    pallas_call x1, Pallas kernels, local(): pl.pallas_call(gather_kernel, out_shape=(pltpu.VMEM((2, ROWS, COLS), bf16...  68.5 us
    pallas_call x1, Pallas kernels, local(): pl.pallas_call(write_kernel, out_shape=(jax.ShapeDtypeStruct((ROWS, COLS)...  6.53 us

profile of v1, /device:TPU:1, one launch (start us, length us, event | category | flops | bytes accessed | tf_op | source)
XLA Modules:
  0.0 75.7 jit_solution(9977995606290049422)
XLA Ops:
  0.6 68.5 %gather.1 = (bf16[2,2048,2048]{2,1,0:T(8,128)(2,1)S(1)}, f32[2,16,128]{2,1,0:T(8,128)S(1)}, f32[8,2,128]{2,1,0:T(2,128)S(1)}) custom-call(f32[32]{0:T(128)} %mix_h.1, f32[32,2048]{1,0:T(8,128)} %one_g.1, f32[32,2048]{1,0:T(8,128)} %other_g.1, f32[32,2048]{1,0:T(8,128)} %one_u.1, f32[32,2048]{1,0:T(8,128)} %other_u.1, f32[8]{0:T(128)} %train_h.1, f32[8]{0:T(128)} %step_h.1), custom_call_target="tpu_custom_call" | custom-call | tf_op jit(solution)/shard_map/gather/pallas_call | solution.py:310
  69.1 6.5 %write.1 = (bf16[2048,2048]{1,0:T(8,128)(2,1)}, bf16[2048,2048]{1,0:T(8,128)(2,1)}, f32[16,128]{1,0:T(8,128)}, f32[16,128]{1,0:T(8,128)}, bf16[16,128]{1,0:T(8,128)(2,1)}) custom-call(bf16[2,2048,2048]{2,1,0:T(8,128)(2,1)S(1)} %get-tuple-element.13.tiles, f32[2,16,128]{2,1,0:T(8,128)S(1)} %get-tuple-element.14.cols, f32[8,2,128]{2,1,0:T(2,128)S(1)} %get-tuple-element.15.norm), custom_call_target="tpu_custom_call" | custom-call | tf_op jit(solution)/shard_map/write/pallas_call | solution.py:349

commit v2 on v1

--- a/solution.py
+++ b/solution.py
@@ -17,7 +17,10 @@
 TILES = COLS // 128
 LOW = -3.0e38
 
-PIECES = (("B", 0, 6, 11), ("B", 1, 11, 16), ("A", 0, 0, 3), ("A", 1, 3, 6))
+PIECES = (("A", 0, "own", 0, 7), ("B", 0, "own", 7, 16), ("A", 1, "other", 0, 6), ("B", 1, "other", 6, 16))
+EARLY = (0, 1, 2)
+LINKS = ("y+", "y-", "z+", "z-")
+STEP = {"y+": (0, 1), "y-": (0, -1), "z+": (1, 0), "z-": (-1, 0)}
 
 
 def reach(half, n):
@@ -42,20 +45,24 @@
     return (along_z if dy == 0 else []) + along_y
 
 
-def arrivals(hop=2.0, turn=0.05, rate=1.0 / 5.6):
-    free = dict.fromkeys(("y+", "y-", "z+", "z-"), 0.0)
-    queue, count, clock, order = [], 0, 0.0, []
+def plan(hop=2.0, turn=0.05, block=5.6):
+    free = dict.fromkeys(LINKS, 0.0)
+    queue, count, clock = [], 0, 0.0
+    first = [(p, 0, 0) for p in range(len(PIECES)) if p not in EARLY]
+    first += [(p, *STEP[link]) for p in EARLY for link in LINKS]
+    order = []
 
     def issue(piece, dz, dy, at):
         nonlocal count
         for link, z, y in forwards(piece, dz, dy):
-            width = (PIECES[piece][3] - PIECES[piece][2]) / TILES
-            free[link] = max(at, free[link]) + width / rate
+            width = (PIECES[piece][4] - PIECES[piece][3]) / TILES / C
+            free[link] = max(at, free[link]) + width * block
             count += 1
             heapq.heappush(queue, (free[link] + hop, count, piece, z, y))
 
-    for piece in range(len(PIECES)):
-        issue(piece, 0, 0, clock)
+    for piece, dz, dy in first:
+        order.append((piece, dz, dy))
+        issue(piece, dz, dy, clock)
         clock += 2 * turn
     while queue:
         at, _, piece, dz, dy = heapq.heappop(queue)
@@ -63,38 +70,35 @@
         order.append((piece, dz, dy))
         issue(piece, dz, dy, clock)
         clock += turn
-    return order
+    return order, clock
 
 
 def gather_kernel(
     mix_h, one_g, other_g, one_u, other_u, train_h, step_h,
     out, cols, norm,
-    mix, train, step, ins, theirs, x, peak, peak_y, peak1, peak_z, peak2,
+    mix, train, step, ins, theirs, x, raw, peak, peak_yc, peak1, peak_z, peak2,
     row0, row_x, row1, row_c, row2, row_y,
-    in_sem, x_sem, peak_send, y_sem, z_sem, col_sem, norm_send, norm_sem,
-    send_sem, recv_sem, side_send, side_recv,
+    in_sem, x_sem, peak_send, yc_sem, z_sem, col_sem, norm_send, norm_sem,
+    raw_send, send_sem, recv_sem, side_send, side_recv,
 ):
-    z, y, c, m = (lax.axis_index(a) for a in ("shard_0", "shard_1", "shard_2", "model"))
-
-    def device(z, y, c, m):
-        return (z, y, c, m)
-
-    z_at = [device(lax.rem(z + d, Z), y, c, m) for d in range(Z)]
-    y_at = [device(z, lax.rem(y + d, Y), c, m) for d in range(Y)]
-    m_at = [device(z, y, c, lax.rem(m + d, X)) for d in range(X)]
-    sibling = device(z, y, 1 - c, m)
+    z, y, c, m = (lax.axis_index(a) for a in SHARD_MODEL)
+    mesh_id = pl.DeviceIdType.MESH
+    z_at = [(lax.rem(z + d, Z), y, c, m) for d in range(Z)]
+    y_at = [(z, lax.rem(y + d, Y), c, m) for d in range(Y)]
+    yo_at = [(z, lax.rem(y + d, Y), 1 - c, m) for d in range(Y)]
+    m_at = [(z, y, c, lax.rem(m + d, X)) for d in range(X)]
+    sibling = yo_at[0]
     link_to = {"z+": z_at[1], "z-": z_at[Z - 1], "y+": y_at[1], "y-": y_at[Y - 1]}
 
     def remote(src, dst, send, recv, to):
         return pltpu.make_async_remote_copy(
-            src_ref=src, dst_ref=dst, send_sem=send, recv_sem=recv,
-            device_id=to, device_id_type=pl.DeviceIdType.MESH,
+            src_ref=src, dst_ref=dst, send_sem=send, recv_sem=recv, device_id=to, device_id_type=mesh_id
         )
 
-    partners = [sibling, *y_at[1:], *z_at[1:], *m_at[1:]]
+    partners = [*yo_at, *y_at[1:], *z_at[1:], *m_at[1:]]
     barrier = pltpu.get_barrier_semaphore()
     for to in partners:
-        pl.semaphore_signal(barrier, inc=1, device_id=to, device_id_type=pl.DeviceIdType.MESH)
+        pl.semaphore_signal(barrier, inc=1, device_id=to, device_id_type=mesh_id)
 
     gate, up = 2 * (1 - c), 2 * c
     small = [
@@ -121,22 +125,29 @@
             share = jnp.where(sub == i, mix[8 * r + i], share)
         shares.append((share, 1.0 - share))
 
-    def blend(slot, store):
+    def blend(slot, to_peak, store):
         for k in (slot, slot + 1):
             pltpu.make_async_copy(one_g, ins.at[k], in_sem.at[k]).wait()
         for t in range(TILES):
             lanes = slice(128 * t, 128 * t + 128)
+            best = None
             for r, (share, rest) in enumerate(shares):
                 rows = slice(8 * r, 8 * r + 8)
-                store(r, lanes, share * ins[slot, rows, lanes] + rest * ins[slot + 1, rows, lanes])
+                value = share * ins[slot, rows, lanes] + rest * ins[slot + 1, rows, lanes]
+                store(r, lanes, value)
+                best = jnp.abs(value) if best is None else jnp.maximum(best, jnp.abs(value))
+            peak[to_peak, t : t + 1, :] = jnp.max(best, axis=0, keepdims=True)
+
+    own_row, other_row = pl.multiple_of(OWN * c, OWN), pl.multiple_of(OWN * (1 - c), OWN)
 
     def store_theirs(r, lanes, value):
         theirs[8 * r : 8 * r + 8, lanes] = value
 
     def store_own(r, lanes, value):
-        x[pl.ds(pl.multiple_of(OWN * c + 8 * r, 8), 8), lanes] = value
-
-    blend(0, store_theirs)
+        x[pl.ds(pl.multiple_of(own_row + 8 * r, 8), 8), lanes] = value
+
+    blend(0, 1, store_theirs)
+    blend(2, 0, store_own)
 
     lane2 = lax.broadcasted_iota(jnp.int32, (2, 128), 1)
     sub2 = lax.broadcasted_iota(jnp.int32, (2, 128), 0)
@@ -148,40 +159,53 @@
 
     pl.semaphore_wait(barrier, len(partners))
 
-    to_sibling = remote(
-        theirs, x.at[pl.ds(pl.multiple_of(OWN * c, OWN), OWN)], x_sem.at[0], x_sem.at[1], sibling
-    )
+    over_yc = [remote(peak.at[1], peak_yc.at[0], peak_send.at[0], yc_sem.at[0], sibling)]
+    for d in range(1, Y):
+        over_yc.append(remote(peak.at[0], peak_yc.at[2 * d - 1], peak_send.at[0], yc_sem.at[2 * d - 1], y_at[d]))
+        over_yc.append(remote(peak.at[1], peak_yc.at[2 * d], peak_send.at[0], yc_sem.at[2 * d], yo_at[d]))
+    for copy in over_yc:
+        copy.start()
+    to_sibling = remote(theirs, x.at[pl.ds(own_row, OWN)], x_sem.at[0], x_sem.at[1], sibling)
     to_sibling.start()
+
+    def flag(piece, dz, dy):
+        return recv_sem.at[piece, (dz % Z) * Y + dy % Y]
+
+    def rows_of(piece):
+        return own_row if PIECES[piece][2] == "own" else other_row
+
+    def lanes_of(piece):
+        first, last = PIECES[piece][3:]
+        return pl.ds(128 * first, 128 * (last - first))
+
+    def early(piece, link):
+        at = (pl.ds(rows_of(piece), OWN), lanes_of(piece))
+        return remote(
+            x.at[at], raw.at[(LINKS.index(link), *at)], raw_send.at[piece], flag(piece, *STEP[link]), link_to[link]
+        )
+
+    for link in LINKS:
+        early(0, link).start()
+    for link in ("y+", "y-"):
+        early(1, link).start()
     norm_x = [remote(row0, row_x.at[d], norm_send.at[0], norm_sem.at[d], m_at[d]) for d in range(1, X)]
     for copy in norm_x:
         copy.start()
-    blend(2, store_own)
-
-    def peak_of(t, first):
-        lanes = slice(128 * t, 128 * t + 128)
-        best = jnp.abs(x[pl.ds(pl.multiple_of(first, 8), 8), lanes])
-        for r in range(1, OWN // 8):
-            best = jnp.maximum(best, jnp.abs(x[pl.ds(pl.multiple_of(first + 8 * r, 8), 8), lanes]))
-        return best
-
-    own_peaks = [peak_of(t, OWN * c) for t in range(TILES)]
+
+    best = peak[0]
+    for d, copy in enumerate(over_yc):
+        copy.wait_recv()
+        best = jnp.maximum(best, peak_yc[d])
+    peak1[...] = best
+
+    over_z = [remote(peak1, peak_z.at[d], peak_send.at[1], z_sem.at[d], z_at[d]) for d in range(1, Z)]
+    for d in sorted(range(1, Z), key=lambda d: -min(d, Z - d)):
+        over_z[d - 1].start()
+    for link in ("z+", "z-"):
+        early(1, link).start()
     to_sibling.wait_recv()
-    for t in range(TILES):
-        best = jnp.maximum(own_peaks[t], peak_of(t, OWN * (1 - c)))
-        peak[t : t + 1, :] = jnp.max(best, axis=0, keepdims=True)
-
-    over_y = [remote(peak, peak_y.at[d], peak_send.at[0], y_sem.at[d], y_at[d]) for d in range(1, Y)]
-    for copy in over_y:
-        copy.start()
-    best = peak[...]
-    for d, copy in enumerate(over_y, 1):
-        copy.wait_recv()
-        best = jnp.maximum(best, peak_y[d])
-    peak1[...] = best
-
-    over_z = [remote(peak1, peak_z.at[d], peak_send.at[1], z_sem.at[d], z_at[d]) for d in range(1, Z)]
-    for copy in over_z:
-        copy.start()
+    for link in LINKS:
+        early(2, link).start()
     for d, copy in enumerate(over_z, 1):
         copy.wait_recv()
         best = jnp.maximum(best, peak_z[d])
@@ -192,41 +216,25 @@
         chip = lax.rem(z - dz + Z, Z) * Y + lax.rem(y - dy + Y, Y)
         return pl.multiple_of(chip * CHIP, CHIP)
 
-    home = block_at(0, 0)
-
-    def scale(piece):
-        for t in range(*PIECES[piece][2:]):
+    def scale(piece, source, base):
+        for t in range(*PIECES[piece][3:]):
             lanes = slice(128 * t, 128 * t + 128)
             by = jnp.broadcast_to(peak2[t : t + 1, :], (16, 128))
-            for r in range(CHIP // 16):
-                rows = pl.ds(pl.multiple_of(home + 16 * r, 16), 16)
-                out[c, rows, lanes] = (x[16 * r : 16 * r + 16, lanes] / by).astype(jnp.bfloat16)
-
-    def flag(piece, dz, dy):
-        return recv_sem.at[piece, (dz % Z) * Y + dy % Y]
-
-    def part(piece, base):
-        first, last = PIECES[piece][2:]
-        return out.at[c, pl.ds(base, CHIP), pl.ds(128 * first, 128 * (last - first))]
+            for r in range(OWN // 16):
+                at = pl.multiple_of(rows_of(piece) + 16 * r, 16)
+                value = source[pl.ds(at, 16), lanes] / by
+                out[c, pl.ds(pl.multiple_of(base + at, 16), 16), lanes] = value.astype(jnp.bfloat16)
 
     def send_on(piece, dz, dy, base):
-        ref = part(piece, base)
+        ref = out.at[c, pl.ds(pl.multiple_of(base + rows_of(piece), OWN), OWN), lanes_of(piece)]
         for link, to_z, to_y in forwards(piece, dz, dy):
-            remote(ref, ref, send_sem.at[0], flag(piece, to_z, to_y), link_to[link]).start()
+            remote(ref, ref, send_sem.at[piece], flag(piece, to_z, to_y), link_to[link]).start()
 
     def send_aside(base):
         ref = out.at[c, pl.ds(base, CHIP)]
         remote(ref, ref, side_send.at[0], side_recv.at[0], sibling).start()
 
-    scale(0)
-    for piece in range(len(PIECES)):
-        if piece + 1 < len(PIECES):
-            scale(piece + 1)
-        send_on(piece, 0, 0, home)
-    send_aside(home)
-    col_copy = remote(cols.at[c], cols.at[c], col_sem.at[0], col_sem.at[1], sibling)
-    col_copy.start()
-
+    home = block_at(0, 0)
     n_wait = {}
 
     def norm_over_x():
@@ -259,27 +267,57 @@
         for copy in n_wait["z"]:
             copy.start()
 
-    aside = {12: norm_over_x, 36: norm_over_core, 64: norm_over_y}
+    def own_rest():
+        for piece in EARLY:
+            scale(piece, x, home)
+        send_aside(home)
+        n_wait["col"] = remote(cols.at[c], cols.at[c], col_sem.at[0], col_sem.at[1], sibling)
+        n_wait["col"].start()
+
+    order, _ = plan()
+    n = len(order)
+    aside = {n // 8: own_rest, n // 6: norm_over_x, n // 3: norm_over_core, n // 2: norm_over_y}
     seen = {}
-    for k, (piece, dz, dy) in enumerate(arrivals()):
+    pending = None
+    for k, (piece, dz, dy) in enumerate(order):
         if k in aside:
             aside[k]()
         base = block_at(dz, dy)
-        ref = part(piece, base)
-        remote(ref, ref, send_sem.at[0], flag(piece, dz, dy), sibling).wait_recv()
-        send_on(piece, dz, dy, base)
-        seen[dz % Z, dy % Y] = seen.get((dz % Z, dy % Y), 0) + 1
-        if seen[dz % Z, dy % Y] == len(PIECES):
-            send_aside(base)
+        computed = (dz, dy) == (0, 0) or (piece in EARLY and abs(dz) + abs(dy) == 1)
+        if (dz, dy) == (0, 0):
+            scale(piece, x, base)
+        elif computed:
+            link = LINKS[[STEP[l] for l in LINKS].index((dz, dy))]
+            early(piece, link).wait_recv()
+            scale(piece, raw.at[LINKS.index(link)], base)
+        else:
+            ref = out.at[c, pl.ds(pl.multiple_of(base + rows_of(piece), OWN), OWN), lanes_of(piece)]
+            remote(ref, ref, send_sem.at[piece], flag(piece, dz, dy), sibling).wait_recv()
+        if pending:
+            send_on(*pending)
+        pending = (piece, dz, dy, base)
+        if not computed:
+            send_on(*pending)
+            pending = None
+        if (dz, dy) != (0, 0):
+            seen[dz % Z, dy % Y] = seen.get((dz % Z, dy % Y), 0) + 1
+            if seen[dz % Z, dy % Y] == len(PIECES):
+                send_aside(base)
 
     for copy in n_wait["z"]:
         copy.wait_recv()
-    col_copy.wait()
+    n_wait["col"].wait()
     to_sibling.wait_send()
-    for copy in norm_x + [n_wait["c"]] + n_wait["y"] + n_wait["z"] + over_y + over_z:
+    for copy in norm_x + [n_wait["c"]] + n_wait["y"] + n_wait["z"] + over_yc + over_z:
         copy.wait_send()
-    others = out.at[0, pl.ds(0, ROWS - CHIP)]
-    pltpu.make_async_copy(others, others, send_sem.at[0]).wait()
+    for piece in range(len(PIECES)):
+        sends = Z * Y - 1
+        if piece in EARLY:
+            sends -= len(LINKS)
+            ref = ins.at[:, :, lanes_of(piece)]
+            pltpu.make_async_copy(ref, ref, raw_send.at[piece]).wait()
+        ref = out.at[0, pl.ds(0, sends * OWN), lanes_of(piece)]
+        pltpu.make_async_copy(ref, ref, send_sem.at[piece]).wait()
     whole = out.at[0]
     pltpu.make_async_copy(whole, whole, side_send.at[0]).wait()
     pltpu.make_async_copy(whole, whole, side_recv.at[0]).wait()
@@ -321,8 +359,9 @@
             pltpu.VMEM((4, OWN, COLS), f32),
             pltpu.VMEM((OWN, COLS), f32),
             pltpu.VMEM((CHIP, COLS), f32),
-            pltpu.VMEM((TILES, 128), f32),
-            pltpu.VMEM((Y, TILES, 128), f32),
+            pltpu.VMEM((len(LINKS), CHIP, COLS), f32),
+            pltpu.VMEM((C, TILES, 128), f32),
+            pltpu.VMEM((C * Y - 1, TILES, 128), f32),
             pltpu.VMEM((TILES, 128), f32),
             pltpu.VMEM((Z, TILES, 128), f32),
             pltpu.VMEM((TILES, 128), f32),
@@ -332,8 +371,8 @@
             pltpu.VMEM((2, 128), f32),
             pltpu.VMEM((2, 128), f32),
             pltpu.VMEM((Y, 2, 128), f32),
-            dma((7,)), dma((2,)), dma((2,)), dma((Y,)), dma((Z,)), dma((2,)), dma((4,)), dma((7 + Z,)),
-            dma((1,)), dma((len(PIECES), Z * Y)), dma((1,)), dma((1,)),
+            dma((7,)), dma((2,)), dma((2,)), dma((C * Y - 1,)), dma((Z,)), dma((2,)), dma((4,)), dma((7 + Z,)),
+            dma((len(PIECES),)), dma((len(PIECES),)), dma((len(PIECES), Z * Y)), dma((1,)), dma((1,)),
         ],
         compiler_params=pltpu.CompilerParams(
             collective_id=0, has_side_effects=True, vmem_limit_bytes=24 * 2**20

time: 75.8 us -> 75.8 us (level)
  no operation moved by 1% of the time
where the time goes in v2:
time: 75.8 us; the launch traced here: 75.7 us
  Pallas kernels  75.1 us (99%)
    pallas_call x1, Pallas kernels, local(): pl.pallas_call(gather_kernel, out_shape=(pltpu.VMEM((2, ROWS, COLS), bf16...  68.5 us
    pallas_call x1, Pallas kernels, local(): pl.pallas_call(write_kernel, out_shape=(jax.ShapeDtypeStruct((ROWS, COLS)...  6.53 us

profile of v2, /device:TPU:1, one launch (start us, length us, event | category | flops | bytes accessed | tf_op | source)
XLA Modules:
  0.0 75.7 jit_solution(12598482560684393075)
XLA Ops:
  0.6 68.5 %gather.1 = (bf16[2,2048,2048]{2,1,0:T(8,128)(2,1)S(1)}, f32[2,16,128]{2,1,0:T(8,128)S(1)}, f32[8,2,128]{2,1,0:T(2,128)S(1)}) custom-call(f32[32]{0:T(128)} %mix_h.1, f32[32,2048]{1,0:T(8,128)} %one_g.1, f32[32,2048]{1,0:T(8,128)} %other_g.1, f32[32,2048]{1,0:T(8,128)} %one_u.1, f32[32,2048]{1,0:T(8,128)} %other_u.1, f32[8]{0:T(128)} %train_h.1, f32[8]{0:T(128)} %step_h.1), custom_call_target="tpu_custom_call" | custom-call | tf_op jit(solution)/shard_map/gather/pallas_call | solution.py:348
  69.2 6.5 %write.1 = (bf16[2048,2048]{1,0:T(8,128)(2,1)}, bf16[2048,2048]{1,0:T(8,128)(2,1)}, f32[16,128]{1,0:T(8,128)}, f32[16,128]{1,0:T(8,128)}, bf16[16,128]{1,0:T(8,128)(2,1)}) custom-call(bf16[2,2048,2048]{2,1,0:T(8,128)(2,1)S(1)} %get-tuple-element.13.tiles, f32[2,16,128]{2,1,0:T(8,128)S(1)} %get-tuple-element.14.cols, f32[8,2,128]{2,1,0:T(2,128)S(1)} %get-tuple-element.15.norm), custom_call_target="tpu_custom_call" | custom-call | tf_op jit(solution)/shard_map/write/pallas_call | solution.py:388

commit v3 on v2

--- a/solution.py
+++ b/solution.py
@@ -16,11 +16,17 @@
 CHIP = C * OWN
 TILES = COLS // 128
 LOW = -3.0e38
-
-PIECES = (("A", 0, "own", 0, 7), ("B", 0, "own", 7, 16), ("A", 1, "other", 0, 6), ("B", 1, "other", 6, 16))
-EARLY = (0, 1, 2)
+LATE = 24
+
+PIECES = (("A", 0, "own", 0, 6), ("B", 0, "own", 6, 16), ("A", 1, "other", 0, 7), ("B", 1, "other", 7, 16))
+FIRST = (3, 1, 0, 2)
+EARLY = {"y": ((0, 2, 1), ()), "z": ((1,), (3,))}
 LINKS = ("y+", "y-", "z+", "z-")
 STEP = {"y+": (0, 1), "y-": (0, -1), "z+": (1, 0), "z-": (-1, 0)}
+
+
+def is_early(piece, link):
+    return any(piece in some for some in EARLY[link[0]])
 
 
 def reach(half, n):
@@ -45,42 +51,87 @@
     return (along_z if dy == 0 else []) + along_y
 
 
-def plan(hop=2.0, turn=0.05, block=5.6):
+def plan(hop=2.0, turn=0.04, block=5.6, swap=1.6, over_y=4.0, letters=0.9, over_z=8.5, work=0.08):
     free = dict.fromkeys(LINKS, 0.0)
-    queue, count, clock = [], 0, 0.0
-    first = [(p, 0, 0) for p in range(len(PIECES)) if p not in EARLY]
-    first += [(p, *STEP[link]) for p in EARLY for link in LINKS]
-    order = []
-
-    def issue(piece, dz, dy, at):
+    queue, order, count = [], [], 0
+
+    def put(piece, link, z, y, at, early=False):
         nonlocal count
-        for link, z, y in forwards(piece, dz, dy):
-            width = (PIECES[piece][4] - PIECES[piece][3]) / TILES / C
-            free[link] = max(at, free[link]) + width * block
-            count += 1
-            heapq.heappush(queue, (free[link] + hop, count, piece, z, y))
-
-    for piece, dz, dy in first:
-        order.append((piece, dz, dy))
-        issue(piece, dz, dy, clock)
-        clock += 2 * turn
+        width = (PIECES[piece][4] - PIECES[piece][3]) / TILES / C
+        free[link] = max(at, free[link]) + width * block * (2 if early else 1)
+        count += 1
+        rank = FIRST.index(piece) if early else len(PIECES)
+        heapq.heappush(queue, (max(free[link] + hop, over_z), rank, count, piece, z, y))
+
+    for k, begin in enumerate((0.0, over_y)):
+        for link in LINKS:
+            for piece in EARLY[link[0]][k]:
+                put(piece, link, *STEP[link], max(begin, swap if PIECES[piece][2] == "other" else 0.0), True)
+        if k == 0:
+            for link in ("z+", "z-"):
+                free[link] = max(free[link], over_y) + letters
+    clock = over_z
+    for piece in range(len(PIECES)):
+        if not all(is_early(piece, link) for link in LINKS):
+            heapq.heappush(queue, (over_z, FIRST.index(piece) - 100, 0, piece, 0, 0))
     while queue:
-        at, _, piece, dz, dy = heapq.heappop(queue)
+        at, _, _, piece, dz, dy = heapq.heappop(queue)
         clock = max(clock, at) + turn
         order.append((piece, dz, dy))
-        issue(piece, dz, dy, clock)
+        links = [l for l in LINKS if STEP[l] == (dz, dy)]
+        if (dz, dy) == (0, 0) or links and is_early(piece, links[0]):
+            clock += work
+        for link, to_z, to_y in forwards(piece, dz, dy):
+            if (dz, dy) != (0, 0) or not is_early(piece, link):
+                put(piece, link, to_z, to_y, clock)
         clock += turn
     return order, clock
+
+
+def came_by(piece, dz, dy):
+    along_z = dz != 0 and (PIECES[piece][0] == "A" or dy == 0)
+    link = ("z" if along_z else "y") + ("+" if (dz if along_z else dy) > 0 else "-")
+    return link, (piece, dz - STEP[link][0], dy - STEP[link][1])
+
+
+def share_flags(order):
+    at = {event: k for k, event in enumerate(order)}
+    known = {link: [-1] * len(order) for link in LINKS}
+    for k, event in enumerate(order):
+        for link in LINKS:
+            known[link][k] = known[link][k - 1] if k else -1
+        if event[1:] != (0, 0):
+            link, before = came_by(*event)
+            if before[1:] != (0, 0) or not is_early(event[0], link):
+                back = link[0] + ("-" if link[1] == "+" else "+")
+                known[back][k] = max(known[back][k], at[before])
+    flags, last = {}, []
+    for k, event in enumerate(order):
+        if event[1:] == (0, 0):
+            continue
+        link, before = came_by(*event)
+        early = before[1:] == (0, 0) and is_early(event[0], link)
+        free = [] if early else [i for i, used in enumerate(last) if used <= known[link][at[before]]]
+        if free:
+            i = min(free, key=lambda i: last[i])
+            last[i] = k
+        else:
+            i = len(last)
+            last.append(k)
+        flags[event] = i
+    return flags, len(last)
 
 
 def gather_kernel(
     mix_h, one_g, other_g, one_u, other_u, train_h, step_h,
     out, cols, norm,
     mix, train, step, ins, theirs, x, raw, peak, peak_yc, peak1, peak_z, peak2,
-    row0, row_x, row1, row_c, row2, row_y,
-    in_sem, x_sem, peak_send, yc_sem, z_sem, col_sem, norm_send, norm_sem,
+    row0, row_x, row1, row2, row_y,
+    in_sem, x_sem, peak_send, yc_sem, z_sem, norm_send, norm_sem,
     raw_send, send_sem, recv_sem, side_send, side_recv,
 ):
+    order, _ = plan()
+    flags, _ = share_flags(order)
     z, y, c, m = (lax.axis_index(a) for a in SHARD_MODEL)
     mesh_id = pl.DeviceIdType.MESH
     z_at = [(lax.rem(z + d, Z), y, c, m) for d in range(Z)]
@@ -100,20 +151,15 @@
     for to in partners:
         pl.semaphore_signal(barrier, inc=1, device_id=to, device_id_type=mesh_id)
 
-    gate, up = 2 * (1 - c), 2 * c
     small = [
-        pltpu.make_async_copy(mix_h, mix, in_sem.at[4]),
-        pltpu.make_async_copy(train_h, train, in_sem.at[5]),
-        pltpu.make_async_copy(step_h, step, in_sem.at[6]),
+        pltpu.make_async_copy(ref, to, in_sem.at[2 + i])
+        for i, (ref, to) in enumerate(((mix_h, mix), (train_h, train), (step_h, step)))
     ]
-    large = [
-        pltpu.make_async_copy(one_g, ins.at[gate], in_sem.at[gate]),
-        pltpu.make_async_copy(other_g, ins.at[gate + 1], in_sem.at[gate + 1]),
-        pltpu.make_async_copy(one_u, ins.at[up], in_sem.at[up]),
-        pltpu.make_async_copy(other_u, ins.at[up + 1], in_sem.at[up + 1]),
-    ]
-    for copy in small + large:
+    for copy in small:
         copy.start()
+    for ours, pair in ((1 - c, (one_g, other_g)), (c, (one_u, other_u))):
+        for k, ref in enumerate(pair):
+            pltpu.make_async_copy(ref, ins.at[2 * ours + k], in_sem.at[ours]).start()
     for copy in small:
         copy.wait()
 
@@ -126,8 +172,8 @@
         shares.append((share, 1.0 - share))
 
     def blend(slot, to_peak, store):
-        for k in (slot, slot + 1):
-            pltpu.make_async_copy(one_g, ins.at[k], in_sem.at[k]).wait()
+        both = ins.at[pl.ds(slot, 2)]
+        pltpu.make_async_copy(both, both, in_sem.at[slot // 2]).wait()
         for t in range(TILES):
             lanes = slice(128 * t, 128 * t + 128)
             best = None
@@ -159,17 +205,24 @@
 
     pl.semaphore_wait(barrier, len(partners))
 
-    over_yc = [remote(peak.at[1], peak_yc.at[0], peak_send.at[0], yc_sem.at[0], sibling)]
-    for d in range(1, Y):
-        over_yc.append(remote(peak.at[0], peak_yc.at[2 * d - 1], peak_send.at[0], yc_sem.at[2 * d - 1], y_at[d]))
-        over_yc.append(remote(peak.at[1], peak_yc.at[2 * d], peak_send.at[0], yc_sem.at[2 * d], yo_at[d]))
+    over_yc = []
+    for d in (2, 1, 3):
+        over_yc.append(remote(peak.at[1], peak_yc.at[2 * d], peak_send.at[0], yc_sem.at[0], yo_at[d]))
+        over_yc.append(remote(peak.at[0], peak_yc.at[2 * d - 1], peak_send.at[0], yc_sem.at[0], y_at[d]))
+    over_yc.append(remote(peak.at[1], peak_yc.at[0], peak_send.at[0], yc_sem.at[0], sibling))
     for copy in over_yc:
         copy.start()
     to_sibling = remote(theirs, x.at[pl.ds(own_row, OWN)], x_sem.at[0], x_sem.at[1], sibling)
     to_sibling.start()
-
-    def flag(piece, dz, dy):
-        return recv_sem.at[piece, (dz % Z) * Y + dy % Y]
+    norm_x = [remote(row0, row_x.at[d], norm_send.at[0], norm_sem.at[0], m_at[d]) for d in range(1, X)]
+    for copy in norm_x:
+        copy.start()
+
+    def arrived(ref, sem):
+        pltpu.make_async_copy(ref, ref, sem).wait()
+
+    def flag(*event):
+        return recv_sem.at[flags[event]]
 
     def rows_of(piece):
         return own_row if PIECES[piece][2] == "own" else other_row
@@ -181,33 +234,34 @@
     def early(piece, link):
         at = (pl.ds(rows_of(piece), OWN), lanes_of(piece))
         return remote(
-            x.at[at], raw.at[(LINKS.index(link), *at)], raw_send.at[piece], flag(piece, *STEP[link]), link_to[link]
+            x.at[at], raw.at[(LINKS.index(link), *at)], raw_send.at[0], flag(piece, *STEP[link]), link_to[link]
         )
 
+    own_first = {}
     for link in LINKS:
-        early(0, link).start()
-    for link in ("y+", "y-"):
-        early(1, link).start()
-    norm_x = [remote(row0, row_x.at[d], norm_send.at[0], norm_sem.at[d], m_at[d]) for d in range(1, X)]
-    for copy in norm_x:
-        copy.start()
-
+        some = [PIECES[piece][2] for piece in EARLY[link[0]][0]] + ["other"]
+        own_first[link] = some.index("other")
+        for piece in EARLY[link[0]][0][: own_first[link]]:
+            early(piece, link).start()
+    to_sibling.wait_recv()
+    for link in LINKS:
+        for piece in EARLY[link[0]][0][own_first[link] :]:
+            early(piece, link).start()
+
+    arrived(peak_yc, yc_sem.at[0])
     best = peak[0]
-    for d, copy in enumerate(over_yc):
-        copy.wait_recv()
+    for d in range(C * Y - 1):
         best = jnp.maximum(best, peak_yc[d])
     peak1[...] = best
 
-    over_z = [remote(peak1, peak_z.at[d], peak_send.at[1], z_sem.at[d], z_at[d]) for d in range(1, Z)]
+    over_z = [remote(peak1, peak_z.at[d], peak_send.at[0], z_sem.at[0], z_at[d]) for d in range(1, Z)]
     for d in sorted(range(1, Z), key=lambda d: -min(d, Z - d)):
         over_z[d - 1].start()
-    for link in ("z+", "z-"):
-        early(1, link).start()
-    to_sibling.wait_recv()
     for link in LINKS:
-        early(2, link).start()
-    for d, copy in enumerate(over_z, 1):
-        copy.wait_recv()
+        for piece in EARLY[link[0]][1]:
+            early(piece, link).start()
+    arrived(peak_z.at[pl.ds(1, Z - 1)], z_sem.at[0])
+    for d in range(1, Z):
         best = jnp.maximum(best, peak_z[d])
     peak2[...] = best
     cols[c] = best
@@ -228,71 +282,67 @@
     def send_on(piece, dz, dy, base):
         ref = out.at[c, pl.ds(pl.multiple_of(base + rows_of(piece), OWN), OWN), lanes_of(piece)]
         for link, to_z, to_y in forwards(piece, dz, dy):
-            remote(ref, ref, send_sem.at[piece], flag(piece, to_z, to_y), link_to[link]).start()
-
-    def send_aside(base):
-        ref = out.at[c, pl.ds(base, CHIP)]
+            if (dz, dy) == (0, 0) and is_early(piece, link):
+                continue
+            remote(ref, ref, send_sem.at[0], flag(piece, to_z, to_y), link_to[link]).start()
+
+    def send_aside(base, rows=CHIP, lanes=pl.ds(0, COLS)):
+        ref = out.at[c, pl.ds(base, rows), lanes]
         remote(ref, ref, side_send.at[0], side_recv.at[0], sibling).start()
 
     home = block_at(0, 0)
-    n_wait = {}
 
     def norm_over_x():
         line = row0[...]
-        for d, copy in enumerate(norm_x, 1):
-            copy.wait_recv()
+        arrived(row_x.at[pl.ds(1, X - 1)], norm_sem.at[0])
+        for d in range(1, X):
             line = jnp.maximum(line, row_x[d])
         row1[...] = line
-        n_wait["c"] = remote(row1, row_c, norm_send.at[1], norm_sem.at[4], sibling)
-        n_wait["c"].start()
+        remote(row1, row_y.at[0], norm_send.at[1], norm_sem.at[1], sibling).start()
 
     def norm_over_core():
-        n_wait["c"].wait_recv()
-        row2[...] = jnp.maximum(row1[...], row_c[...])
-        n_wait["y"] = [
-            remote(row2, row_y.at[d], norm_send.at[2], norm_sem.at[4 + d], y_at[d]) for d in range(1, Y)
-        ]
-        for copy in n_wait["y"]:
-            copy.start()
+        arrived(row_y.at[0], norm_sem.at[1])
+        row2[...] = jnp.maximum(row1[...], row_y[0])
+        for d in range(1, Y):
+            remote(row2, row_y.at[d], norm_send.at[1], norm_sem.at[2], y_at[d]).start()
 
     def norm_over_y():
         line = row2[...]
-        for d, copy in enumerate(n_wait["y"], 1):
-            copy.wait_recv()
+        arrived(row_y.at[pl.ds(1, Y - 1)], norm_sem.at[2])
+        for d in range(1, Y):
             line = jnp.maximum(line, row_y[d])
         norm[z] = line
-        n_wait["z"] = [
-            remote(norm.at[z], norm.at[z], norm_send.at[3], norm_sem.at[7 + d], z_at[d]) for d in range(1, Z)
-        ]
-        for copy in n_wait["z"]:
-            copy.start()
+        for d in range(1, Z):
+            remote(norm.at[z], norm.at[z], norm_send.at[2], norm_sem.at[3], z_at[d]).start()
 
     def own_rest():
-        for piece in EARLY:
-            scale(piece, x, home)
+        for piece in range(len(PIECES)):
+            if (piece, 0, 0) not in order:
+                scale(piece, x, home)
         send_aside(home)
-        n_wait["col"] = remote(cols.at[c], cols.at[c], col_sem.at[0], col_sem.at[1], sibling)
-        n_wait["col"].start()
-
-    order, _ = plan()
+        remote(cols.at[c], cols.at[c], side_send.at[1], side_recv.at[1], sibling).start()
+
     n = len(order)
     aside = {n // 8: own_rest, n // 6: norm_over_x, n // 3: norm_over_core, n // 2: norm_over_y}
-    seen = {}
+    blocks = {}
+    for k, (_, dz, dy) in enumerate(order):
+        blocks.setdefault((dz % Z, dy % Y), []).append(k)
+    blocks.pop((0, 0), None)
     pending = None
     for k, (piece, dz, dy) in enumerate(order):
         if k in aside:
             aside[k]()
         base = block_at(dz, dy)
-        computed = (dz, dy) == (0, 0) or (piece in EARLY and abs(dz) + abs(dy) == 1)
+        link = next((l for l in LINKS if STEP[l] == (dz, dy)), None)
+        computed = (dz, dy) == (0, 0) or link is not None and is_early(piece, link)
         if (dz, dy) == (0, 0):
             scale(piece, x, base)
         elif computed:
-            link = LINKS[[STEP[l] for l in LINKS].index((dz, dy))]
             early(piece, link).wait_recv()
             scale(piece, raw.at[LINKS.index(link)], base)
         else:
             ref = out.at[c, pl.ds(pl.multiple_of(base + rows_of(piece), OWN), OWN), lanes_of(piece)]
-            remote(ref, ref, send_sem.at[piece], flag(piece, dz, dy), sibling).wait_recv()
+            remote(ref, ref, send_sem.at[0], flag(piece, dz, dy), sibling).wait_recv()
         if pending:
             send_on(*pending)
         pending = (piece, dz, dy, base)
@@ -300,27 +350,27 @@
             send_on(*pending)
             pending = None
         if (dz, dy) != (0, 0):
-            seen[dz % Z, dy % Y] = seen.get((dz % Z, dy % Y), 0) + 1
-            if seen[dz % Z, dy % Y] == len(PIECES):
+            last = blocks[dz % Z, dy % Y][-1]
+            if last >= n - LATE:
+                send_aside(pl.multiple_of(base + rows_of(piece), OWN), OWN, lanes_of(piece))
+            elif last == k:
                 send_aside(base)
 
-    for copy in n_wait["z"]:
-        copy.wait_recv()
-    n_wait["col"].wait()
+    arrived(norm.at[pl.ds(0, Z - 1)], norm_sem.at[3])
+    arrived(cols.at[0], side_send.at[1])
+    arrived(cols.at[0], side_recv.at[1])
     to_sibling.wait_send()
-    for copy in norm_x + [n_wait["c"]] + n_wait["y"] + n_wait["z"] + over_yc + over_z:
-        copy.wait_send()
-    for piece in range(len(PIECES)):
-        sends = Z * Y - 1
-        if piece in EARLY:
-            sends -= len(LINKS)
-            ref = ins.at[:, :, lanes_of(piece)]
-            pltpu.make_async_copy(ref, ref, raw_send.at[piece]).wait()
-        ref = out.at[0, pl.ds(0, sends * OWN), lanes_of(piece)]
-        pltpu.make_async_copy(ref, ref, send_sem.at[piece]).wait()
+    arrived(row_x.at[pl.ds(1, X - 1)], norm_send.at[0])
+    arrived(row_y, norm_send.at[1])
+    arrived(norm.at[pl.ds(0, Z - 1)], norm_send.at[2])
+    arrived(theirs.at[:, pl.ds(0, 64 * (C * Y + Z - 2))], peak_send.at[0])
+    wide = [last - first for _, _, _, first, last in PIECES]
+    soon = [sum(is_early(piece, link) for link in LINKS) for piece in range(len(PIECES))]
+    arrived(out.at[0, pl.ds(0, 16 * sum(a * b for a, b in zip(soon, wide))), pl.ds(0, 512)], raw_send.at[0])
+    arrived(out.at[0, pl.ds(0, 2 * sum((Z * Y - 1 - a) * b for a, b in zip(soon, wide)))], send_sem.at[0])
     whole = out.at[0]
-    pltpu.make_async_copy(whole, whole, side_send.at[0]).wait()
-    pltpu.make_async_copy(whole, whole, side_recv.at[0]).wait()
+    arrived(whole, side_send.at[0])
+    arrived(whole, side_recv.at[0])
 
 
 def write_kernel(tiles, cols, norm, gate, up, col_gate, col_up, gain, sem):
@@ -369,10 +419,9 @@
             pltpu.VMEM((X, 2, 128), f32),
             pltpu.VMEM((2, 128), f32),
             pltpu.VMEM((2, 128), f32),
-            pltpu.VMEM((2, 128), f32),
             pltpu.VMEM((Y, 2, 128), f32),
-            dma((7,)), dma((2,)), dma((2,)), dma((C * Y - 1,)), dma((Z,)), dma((2,)), dma((4,)), dma((7 + Z,)),
-            dma((len(PIECES),)), dma((len(PIECES),)), dma((len(PIECES), Z * Y)), dma((1,)), dma((1,)),
+            dma((5,)), dma((2,)), dma((1,)), dma((1,)), dma((1,)), dma((3,)), dma((4,)),
+            dma((1,)), dma((1,)), dma((share_flags(plan()[0])[1],)), dma((2,)), dma((2,)),
         ],
         compiler_params=pltpu.CompilerParams(
             collective_id=0, has_side_effects=True, vmem_limit_bytes=24 * 2**20

time: 75.8 us -> 71.6 us (0.945)
  Pallas kernels: 75.1 us -> 70.9 us
    pallas_call x1, Pallas kernels: 68.5 us -> 64.3 us  [local(): pl.pallas_call(gather_kernel, out_shape=(pltpu.VMEM((2, ROWS, COLS), bf16...]
where the time goes in v3:
time: 71.6 us; the launch traced here: 71.5 us
  Pallas kernels  70.9 us (99%)
    pallas_call x1, Pallas kernels, local(): pl.pallas_call(gather_kernel, out_shape=(pltpu.VMEM((2, ROWS, COLS), bf16...  64.3 us
    pallas_call x1, Pallas kernels, local(): pl.pallas_call(write_kernel, out_shape=(jax.ShapeDtypeStruct((ROWS, COLS)...  6.53 us

profile of v3, /device:TPU:1, one launch (start us, length us, event | category | flops | bytes accessed | tf_op | source)
XLA Modules:
  0.0 71.5 jit_solution(2035139346903280063)
XLA Ops:
  0.6 64.3 %gather.1 = (bf16[2,2048,2048]{2,1,0:T(8,128)(2,1)S(1)}, f32[2,16,128]{2,1,0:T(8,128)S(1)}, f32[8,2,128]{2,1,0:T(2,128)S(1)}) custom-call(f32[32]{0:T(128)} %mix_h.1, f32[32,2048]{1,0:T(8,128)} %one_g.1, f32[32,2048]{1,0:T(8,128)} %other_g.1, f32[32,2048]{1,0:T(8,128)} %one_u.1, f32[32,2048]{1,0:T(8,128)} %other_u.1, f32[8]{0:T(128)} %train_h.1, f32[8]{0:T(128)} %step_h.1), custom_call_target="tpu_custom_call" | custom-call | tf_op jit(solution)/shard_map/gather/pallas_call | solution.py:398
  65.0 6.5 %write.1 = (bf16[2048,2048]{1,0:T(8,128)(2,1)}, bf16[2048,2048]{1,0:T(8,128)(2,1)}, f32[16,128]{1,0:T(8,128)}, f32[16,128]{1,0:T(8,128)}, bf16[16,128]{1,0:T(8,128)(2,1)}) custom-call(bf16[2,2048,2048]{2,1,0:T(8,128)(2,1)S(1)} %get-tuple-element.13.tiles, f32[2,16,128]{2,1,0:T(8,128)S(1)} %get-tuple-element.14.cols, f32[8,2,128]{2,1,0:T(2,128)S(1)} %get-tuple-element.15.norm), custom_call_target="tpu_custom_call" | custom-call | tf_op jit(solution)/shard_map/write/pallas_call | solution.py:437

commit v4 on v3

--- a/solution.py
+++ b/solution.py
@@ -126,9 +126,9 @@
     mix_h, one_g, other_g, one_u, other_u, train_h, step_h,
     out, cols, norm,
     mix, train, step, ins, theirs, x, raw, peak, peak_yc, peak1, peak_z, peak2,
-    row0, row_x, row1, row2, row_y,
+    row0, row_yc, rows_z, rows_x,
     in_sem, x_sem, peak_send, yc_sem, z_sem, norm_send, norm_sem,
-    raw_send, send_sem, recv_sem, side_send, side_recv,
+    raw_send, send_sem, recv_sem, side_send, side_recv, known,
 ):
     order, _ = plan()
     flags, _ = share_flags(order)
@@ -146,7 +146,7 @@
             src_ref=src, dst_ref=dst, send_sem=send, recv_sem=recv, device_id=to, device_id_type=mesh_id
         )
 
-    partners = [*yo_at, *y_at[1:], *z_at[1:], *m_at[1:]]
+    partners = [*yo_at, *y_at[1:], z_at[1], z_at[Z - 1], *m_at[1:]]
     barrier = pltpu.get_barrier_semaphore()
     for to in partners:
         pl.semaphore_signal(barrier, inc=1, device_id=to, device_id_type=mesh_id)
@@ -214,9 +214,18 @@
         copy.start()
     to_sibling = remote(theirs, x.at[pl.ds(own_row, OWN)], x_sem.at[0], x_sem.at[1], sibling)
     to_sibling.start()
-    norm_x = [remote(row0, row_x.at[d], norm_send.at[0], norm_sem.at[0], m_at[d]) for d in range(1, X)]
-    for copy in norm_x:
-        copy.start()
+    for d in (2, 1, 3):
+        remote(row0, row_yc.at[2 * d], norm_send.at[0], norm_sem.at[0], yo_at[d]).start()
+        remote(row0, row_yc.at[2 * d - 1], norm_send.at[0], norm_sem.at[0], y_at[d]).start()
+    remote(row0, row_yc.at[0], norm_send.at[0], norm_sem.at[0], sibling).start()
+
+    def tell_z():
+        for way, to in enumerate((z_at[1], z_at[Z - 1])):
+            pl.semaphore_signal(known.at[way], inc=1, device_id=to, device_id_type=mesh_id)
+
+    def hear_z():
+        for way in range(2):
+            pl.semaphore_wait(known.at[way], 1)
 
     def arrived(ref, sem):
         pltpu.make_async_copy(ref, ref, sem).wait()
@@ -243,10 +252,17 @@
         own_first[link] = some.index("other")
         for piece in EARLY[link[0]][0][: own_first[link]]:
             early(piece, link).start()
+    tell_z()
+    hear_z()
+    tell_z()
     to_sibling.wait_recv()
     for link in LINKS:
         for piece in EARLY[link[0]][0][own_first[link] :]:
             early(piece, link).start()
+    for _ in range(Z // 2 - 3):
+        hear_z()
+        tell_z()
+    hear_z()
 
     arrived(peak_yc, yc_sem.at[0])
     best = peak[0]
@@ -257,6 +273,13 @@
     over_z = [remote(peak1, peak_z.at[d], peak_send.at[0], z_sem.at[0], z_at[d]) for d in range(1, Z)]
     for d in sorted(range(1, Z), key=lambda d: -min(d, Z - d)):
         over_z[d - 1].start()
+    arrived(row_yc, norm_sem.at[0])
+    line = row0[...]
+    for d in range(C * Y - 1):
+        line = jnp.maximum(line, row_yc[d])
+    rows_z[z] = line
+    for d in range(1, Z):
+        remote(rows_z.at[z], rows_z.at[z], norm_send.at[1], norm_sem.at[1], z_at[d]).start()
     for link in LINKS:
         for piece in EARLY[link[0]][1]:
             early(piece, link).start()
@@ -293,27 +316,17 @@
     home = block_at(0, 0)
 
     def norm_over_x():
-        line = row0[...]
-        arrived(row_x.at[pl.ds(1, X - 1)], norm_sem.at[0])
+        arrived(rows_z.at[pl.ds(0, Z - 1)], norm_sem.at[1])
         for d in range(1, X):
-            line = jnp.maximum(line, row_x[d])
-        row1[...] = line
-        remote(row1, row_y.at[0], norm_send.at[1], norm_sem.at[1], sibling).start()
-
-    def norm_over_core():
-        arrived(row_y.at[0], norm_sem.at[1])
-        row2[...] = jnp.maximum(row1[...], row_y[0])
-        for d in range(1, Y):
-            remote(row2, row_y.at[d], norm_send.at[1], norm_sem.at[2], y_at[d]).start()
-
-    def norm_over_y():
-        line = row2[...]
-        arrived(row_y.at[pl.ds(1, Y - 1)], norm_sem.at[2])
-        for d in range(1, Y):
-            line = jnp.maximum(line, row_y[d])
-        norm[z] = line
-        for d in range(1, Z):
-            remote(norm.at[z], norm.at[z], norm_send.at[2], norm_sem.at[3], z_at[d]).start()
+            remote(rows_z, rows_x.at[d], norm_send.at[2], norm_sem.at[2], m_at[d]).start()
+
+    def norm_done():
+        arrived(rows_x.at[pl.ds(1, X - 1)], norm_sem.at[2])
+        for k in range(Z):
+            line = rows_z[k]
+            for d in range(1, X):
+                line = jnp.maximum(line, rows_x[d, k])
+            norm[k] = line
 
     def own_rest():
         for piece in range(len(PIECES)):
@@ -323,7 +336,7 @@
         remote(cols.at[c], cols.at[c], side_send.at[1], side_recv.at[1], sibling).start()
 
     n = len(order)
-    aside = {n // 8: own_rest, n // 6: norm_over_x, n // 3: norm_over_core, n // 2: norm_over_y}
+    aside = {n // 8: own_rest, n // 4: norm_over_x, n // 2: norm_done}
     blocks = {}
     for k, (_, dz, dy) in enumerate(order):
         blocks.setdefault((dz % Z, dy % Y), []).append(k)
@@ -356,13 +369,12 @@
             elif last == k:
                 send_aside(base)
 
-    arrived(norm.at[pl.ds(0, Z - 1)], norm_sem.at[3])
     arrived(cols.at[0], side_send.at[1])
     arrived(cols.at[0], side_recv.at[1])
     to_sibling.wait_send()
-    arrived(row_x.at[pl.ds(1, X - 1)], norm_send.at[0])
-    arrived(row_y, norm_send.at[1])
-    arrived(norm.at[pl.ds(0, Z - 1)], norm_send.at[2])
+    arrived(row_yc, norm_send.at[0])
+    arrived(rows_z.at[pl.ds(0, Z - 1)], norm_send.at[1])
+    arrived(rows_x.at[pl.ds(1, X - 1)], norm_send.at[2])
     arrived(theirs.at[:, pl.ds(0, 64 * (C * Y + Z - 2))], peak_send.at[0])
     wide = [last - first for _, _, _, first, last in PIECES]
     soon = [sum(is_early(piece, link) for link in LINKS) for piece in range(len(PIECES))]
@@ -416,12 +428,12 @@
             pltpu.VMEM((Z, TILES, 128), f32),
             pltpu.VMEM((TILES, 128), f32),
             pltpu.VMEM((2, 128), f32),
-            pltpu.VMEM((X, 2, 128), f32),
-            pltpu.VMEM((2, 128), f32),
-            pltpu.VMEM((2, 128), f32),
-            pltpu.VMEM((Y, 2, 128), f32),
-            dma((5,)), dma((2,)), dma((1,)), dma((1,)), dma((1,)), dma((3,)), dma((4,)),
+            pltpu.VMEM((C * Y - 1, 2, 128), f32),
+            pltpu.VMEM((Z, 2, 128), f32),
+            pltpu.VMEM((X, Z, 2, 128), f32),
+            dma((5,)), dma((2,)), dma((1,)), dma((1,)), dma((1,)), dma((3,)), dma((3,)),
             dma((1,)), dma((1,)), dma((share_flags(plan()[0])[1],)), dma((2,)), dma((2,)),
+            pltpu.SemaphoreType.REGULAR((2,)),
         ],
         compiler_params=pltpu.CompilerParams(
             collective_id=0, has_side_effects=True, vmem_limit_bytes=24 * 2**20

time: 71.6 us -> 72.5 us (1.013)
  Pallas kernels: 70.9 us -> 71.8 us
    pallas_call x1, Pallas kernels: 64.3 us -> 65.2 us  [local(): pl.pallas_call(gather_kernel, out_shape=(pltpu.VMEM((2, ROWS, COLS), bf16...]
where the time goes in v4:
time: 72.5 us; the launch traced here: 72.4 us
  Pallas kernels  71.8 us (99%)
    pallas_call x1, Pallas kernels, local(): pl.pallas_call(gather_kernel, out_shape=(pltpu.VMEM((2, ROWS, COLS), bf16...  65.2 us
    pallas_call x1, Pallas kernels, local(): pl.pallas_call(write_kernel, out_shape=(jax.ShapeDtypeStruct((ROWS, COLS)...  6.53 us

profile of v4, /device:TPU:1, one launch (start us, length us, event | category | flops | bytes accessed | tf_op | source)
XLA Modules:
  0.0 72.4 jit_solution(11935928125348975959)
XLA Ops:
  0.6 65.2 %gather.1 = (bf16[2,2048,2048]{2,1,0:T(8,128)(2,1)S(1)}, f32[2,16,128]{2,1,0:T(8,128)S(1)}, f32[8,2,128]{2,1,0:T(2,128)S(1)}) custom-call(f32[32]{0:T(128)} %mix_h.1, f32[32,2048]{1,0:T(8,128)} %one_g.1, f32[32,2048]{1,0:T(8,128)} %other_g.1, f32[32,2048]{1,0:T(8,128)} %one_u.1, f32[32,2048]{1,0:T(8,128)} %other_u.1, f32[8]{0:T(128)} %train_h.1, f32[8]{0:T(128)} %step_h.1), custom_call_target="tpu_custom_call" | custom-call | tf_op jit(solution)/shard_map/gather/pallas_call | solution.py:410
  65.9 6.5 %write.1 = (bf16[2048,2048]{1,0:T(8,128)(2,1)}, bf16[2048,2048]{1,0:T(8,128)(2,1)}, f32[16,128]{1,0:T(8,128)}, f32[16,128]{1,0:T(8,128)}, bf16[16,128]{1,0:T(8,128)(2,1)}) custom-call(bf16[2,2048,2048]{2,1,0:T(8,128)(2,1)S(1)} %get-tuple-element.13.tiles, f32[2,16,128]{2,1,0:T(8,128)S(1)} %get-tuple-element.14.cols, f32[8,2,128]{2,1,0:T(2,128)S(1)} %get-tuple-element.15.norm), custom_call_target="tpu_custom_call" | custom-call | tf_op jit(solution)/shard_map/write/pallas_call | solution.py:449

commit v5 on v4

--- a/solution.py
+++ b/solution.py
@@ -146,7 +146,7 @@
             src_ref=src, dst_ref=dst, send_sem=send, recv_sem=recv, device_id=to, device_id_type=mesh_id
         )
 
-    partners = [*yo_at, *y_at[1:], z_at[1], z_at[Z - 1], *m_at[1:]]
+    partners = [*yo_at, *y_at[1:], *(z_at[d] for d in (1, 2, Z - 2, Z - 1)), *m_at[1:]]
     barrier = pltpu.get_barrier_semaphore()
     for to in partners:
         pl.semaphore_signal(barrier, inc=1, device_id=to, device_id_type=mesh_id)
@@ -204,6 +204,9 @@
     row0[...] = line
 
     pl.semaphore_wait(barrier, len(partners))
+
+    for way, to in enumerate((z_at[2], z_at[Z - 2])):
+        pl.semaphore_signal(known.at[way], inc=1, device_id=to, device_id_type=mesh_id)
 
     over_yc = []
     for d in (2, 1, 3):
@@ -219,14 +222,6 @@
         remote(row0, row_yc.at[2 * d - 1], norm_send.at[0], norm_sem.at[0], y_at[d]).start()
     remote(row0, row_yc.at[0], norm_send.at[0], norm_sem.at[0], sibling).start()
 
-    def tell_z():
-        for way, to in enumerate((z_at[1], z_at[Z - 1])):
-            pl.semaphore_signal(known.at[way], inc=1, device_id=to, device_id_type=mesh_id)
-
-    def hear_z():
-        for way in range(2):
-            pl.semaphore_wait(known.at[way], 1)
-
     def arrived(ref, sem):
         pltpu.make_async_copy(ref, ref, sem).wait()
 
@@ -252,17 +247,10 @@
         own_first[link] = some.index("other")
         for piece in EARLY[link[0]][0][: own_first[link]]:
             early(piece, link).start()
-    tell_z()
-    hear_z()
-    tell_z()
     to_sibling.wait_recv()
     for link in LINKS:
         for piece in EARLY[link[0]][0][own_first[link] :]:
             early(piece, link).start()
-    for _ in range(Z // 2 - 3):
-        hear_z()
-        tell_z()
-    hear_z()
 
     arrived(peak_yc, yc_sem.at[0])
     best = peak[0]
@@ -270,6 +258,8 @@
         best = jnp.maximum(best, peak_yc[d])
     peak1[...] = best
 
+    for way in range(2):
+        pl.semaphore_wait(known.at[way], 1)
     over_z = [remote(peak1, peak_z.at[d], peak_send.at[0], z_sem.at[0], z_at[d]) for d in range(1, Z)]
     for d in sorted(range(1, Z), key=lambda d: -min(d, Z - d)):
         over_z[d - 1].start()
@@ -386,7 +376,7 @@
 
 
 def write_kernel(tiles, cols, norm, gate, up, col_gate, col_up, gain, sem):
-    parts = 4
+    parts = 8
     rows = ROWS // parts
     copies = []
     for i, ref in enumerate((gate, up)):
@@ -457,7 +447,7 @@
         ),
         in_specs=[vmem_spec] * 3,
         out_specs=(hbm_spec, hbm_spec, vmem_spec, vmem_spec, vmem_spec),
-        scratch_shapes=[dma((8,))],
+        scratch_shapes=[dma((16,))],
         compiler_params=pltpu.CompilerParams(vmem_limit_bytes=8 * 2**20),
         name="write",
     )(tiles, cols, norm)

time: 72.5 us -> 71.7 us (0.989)
  Pallas kernels: 71.8 us -> 70.9 us
    pallas_call x1, Pallas kernels: 65.2 us -> 64.4 us  [local(): pl.pallas_call(gather_kernel, out_shape=(pltpu.VMEM((2, ROWS, COLS), bf16...]
where the time goes in v5:
time: 71.7 us; the launch traced here: 71.6 us
  Pallas kernels  70.9 us (99%)
    pallas_call x1, Pallas kernels, local(): pl.pallas_call(gather_kernel, out_shape=(pltpu.VMEM((2, ROWS, COLS), bf16...  64.4 us
    pallas_call x1, Pallas kernels, local(): pl.pallas_call(write_kernel, out_shape=(jax.ShapeDtypeStruct((ROWS, COLS)...  6.57 us

profile of v5, /device:TPU:1, one launch (start us, length us, event | category | flops | bytes accessed | tf_op | source)
XLA Modules:
  0.0 71.6 jit_solution(5449689976592261799)
XLA Ops:
  0.6 64.4 %gather.1 = (bf16[2,2048,2048]{2,1,0:T(8,128)(2,1)S(1)}, f32[2,16,128]{2,1,0:T(8,128)S(1)}, f32[8,2,128]{2,1,0:T(2,128)S(1)}) custom-call(f32[32]{0:T(128)} %mix_h.1, f32[32,2048]{1,0:T(8,128)} %one_g.1, f32[32,2048]{1,0:T(8,128)} %other_g.1, f32[32,2048]{1,0:T(8,128)} %one_u.1, f32[32,2048]{1,0:T(8,128)} %other_u.1, f32[8]{0:T(128)} %train_h.1, f32[8]{0:T(128)} %step_h.1), custom_call_target="tpu_custom_call" | custom-call | tf_op jit(solution)/shard_map/gather/pallas_call | solution.py:400
  65.0 6.6 %write.1 = (bf16[2048,2048]{1,0:T(8,128)(2,1)}, bf16[2048,2048]{1,0:T(8,128)(2,1)}, f32[16,128]{1,0:T(8,128)}, f32[16,128]{1,0:T(8,128)}, bf16[16,128]{1,0:T(8,128)(2,1)}) custom-call(bf16[2,2048,2048]{2,1,0:T(8,128)(2,1)S(1)} %get-tuple-element.13.tiles, f32[2,16,128]{2,1,0:T(8,128)S(1)} %get-tuple-element.14.cols, f32[8,2,128]{2,1,0:T(2,128)S(1)} %get-tuple-element.15.norm), custom_call_target="tpu_custom_call" | custom-call | tf_op jit(solution)/shard_map/write/pallas_call | solution.py:439

commit v6 on v5

--- a/solution.py
+++ b/solution.py
@@ -146,7 +146,8 @@
             src_ref=src, dst_ref=dst, send_sem=send, recv_sem=recv, device_id=to, device_id_type=mesh_id
         )
 
-    partners = [*yo_at, *y_at[1:], *(z_at[d] for d in (1, 2, Z - 2, Z - 1)), *m_at[1:]]
+    partners = [z_at[2], z_at[Z - 2], yo_at[2], y_at[2], *(z_at[d] for d in (1, Z - 1)), *(yo_at[d] for d in (1, 3))]
+    partners += [y_at[1], y_at[3], sibling, *m_at[1:]]
     barrier = pltpu.get_barrier_semaphore()
     for to in partners:
         pl.semaphore_signal(barrier, inc=1, device_id=to, device_id_type=mesh_id)
@@ -375,19 +376,21 @@
     arrived(whole, side_recv.at[0])
 
 
-def write_kernel(tiles, cols, norm, gate, up, col_gate, col_up, gain, sem):
-    parts = 8
+def write_kernel(tiles, cols, norm, gate, up, col_gate, col_up, gain, narrow, sem):
+    parts = 4
     rows = ROWS // parts
     copies = []
     for i, ref in enumerate((gate, up)):
         for k in range(parts):
             at = pl.ds(k * rows, rows)
             copies.append(pltpu.make_async_copy(tiles.at[i, at], ref.at[at], sem.at[i * parts + k]))
+    copies.append(pltpu.make_async_copy(cols.at[0], col_gate, sem.at[2 * parts]))
+    copies.append(pltpu.make_async_copy(cols.at[1], col_up, sem.at[2 * parts + 1]))
     for copy in copies:
         copy.start()
-    col_gate[...] = cols[0]
-    col_up[...] = cols[1]
-    gain[...] = jnp.concatenate([norm[k] for k in range(Z)], axis=0).astype(jnp.bfloat16)
+    narrow[...] = jnp.concatenate([norm[k] for k in range(Z)], axis=0).astype(jnp.bfloat16)
+    copies.append(pltpu.make_async_copy(narrow, gain, sem.at[2 * parts + 2]))
+    copies[-1].start()
     for copy in copies:
         copy.wait()
 
@@ -446,8 +449,8 @@
             jax.ShapeDtypeStruct((2 * Z, 128), bf16),
         ),
         in_specs=[vmem_spec] * 3,
-        out_specs=(hbm_spec, hbm_spec, vmem_spec, vmem_spec, vmem_spec),
-        scratch_shapes=[dma((16,))],
+        out_specs=(hbm_spec,) * 5,
+        scratch_shapes=[pltpu.VMEM((2 * Z, 128), bf16), dma((11,))],
         compiler_params=pltpu.CompilerParams(vmem_limit_bytes=8 * 2**20),
         name="write",
     )(tiles, cols, norm)

time: 71.7 us -> 71.1 us (level)
  no operation moved by 1% of the time
where the time goes in v6:
time: 71.1 us; the launch traced here: 71 us
  Pallas kernels  70.3 us (99%)
    pallas_call x1, Pallas kernels, local(): pl.pallas_call(gather_kernel, out_shape=(pltpu.VMEM((2, ROWS, COLS), bf16...  64.4 us
    pallas_call x1, Pallas kernels, local(): pl.pallas_call(write_kernel, out_shape=(jax.ShapeDtypeStruct((ROWS, COLS)...  5.96 us

profile of v6, /device:TPU:1, one launch (start us, length us, event | category | flops | bytes accessed | tf_op | source)
XLA Modules:
  0.0 71.0 jit_solution(16815593047917791813)
XLA Ops:
  0.6 64.4 %gather.1 = (bf16[2,2048,2048]{2,1,0:T(8,128)(2,1)S(1)}, f32[2,16,128]{2,1,0:T(8,128)S(1)}, f32[8,2,128]{2,1,0:T(2,128)S(1)}) custom-call(f32[32]{0:T(128)} %mix_h.1, f32[32,2048]{1,0:T(8,128)} %one_g.1, f32[32,2048]{1,0:T(8,128)} %other_g.1, f32[32,2048]{1,0:T(8,128)} %one_u.1, f32[32,2048]{1,0:T(8,128)} %other_u.1, f32[8]{0:T(128)} %train_h.1, f32[8]{0:T(128)} %step_h.1), custom_call_target="tpu_custom_call" | custom-call | tf_op jit(solution)/shard_map/gather/pallas_call | solution.py:403
  65.0 6.0 %write.1 = (bf16[2048,2048]{1,0:T(8,128)(2,1)}, bf16[2048,2048]{1,0:T(8,128)(2,1)}, f32[16,128]{1,0:T(8,128)}, f32[16,128]{1,0:T(8,128)}, bf16[16,128]{1,0:T(8,128)(2,1)}) custom-call(bf16[2,2048,2048]{2,1,0:T(8,128)(2,1)S(1)} %get-tuple-element.13.tiles, f32[2,16,128]{2,1,0:T(8,128)S(1)} %get-tuple-element.14.cols, f32[8,2,128]{2,1,0:T(2,128)S(1)} %get-tuple-element.15.norm), custom_call_target="tpu_custom_call" | custom-call | tf_op jit(solution)/shard_map/write/pallas_call | solution.py:442

commit v7 on v6

--- a/solution.py
+++ b/solution.py
@@ -147,7 +147,7 @@
         )
 
     partners = [z_at[2], z_at[Z - 2], yo_at[2], y_at[2], *(z_at[d] for d in (1, Z - 1)), *(yo_at[d] for d in (1, 3))]
-    partners += [y_at[1], y_at[3], sibling, *m_at[1:]]
+    partners += [y_at[1], y_at[3], sibling, m_at[1], m_at[X - 1]]
     barrier = pltpu.get_barrier_semaphore()
     for to in partners:
         pl.semaphore_signal(barrier, inc=1, device_id=to, device_id_type=mesh_id)
@@ -306,13 +306,17 @@
 
     home = block_at(0, 0)
 
-    def norm_over_x():
+    def norm_beside():
         arrived(rows_z.at[pl.ds(0, Z - 1)], norm_sem.at[1])
-        for d in range(1, X):
+        for d in (1, X - 1):
             remote(rows_z, rows_x.at[d], norm_send.at[2], norm_sem.at[2], m_at[d]).start()
 
+    def norm_across():
+        arrived(rows_x.at[pl.ds(0, 2)], norm_sem.at[2])
+        remote(rows_x.at[1], rows_x.at[2], norm_send.at[2], norm_sem.at[3], m_at[1]).start()
+
     def norm_done():
-        arrived(rows_x.at[pl.ds(1, X - 1)], norm_sem.at[2])
+        arrived(rows_x.at[2], norm_sem.at[3])
         for k in range(Z):
             line = rows_z[k]
             for d in range(1, X):
@@ -327,7 +331,7 @@
         remote(cols.at[c], cols.at[c], side_send.at[1], side_recv.at[1], sibling).start()
 
     n = len(order)
-    aside = {n // 8: own_rest, n // 4: norm_over_x, n // 2: norm_done}
+    aside = {n // 8: own_rest, n // 4: norm_beside, n // 2: norm_across, 3 * n // 4: norm_done}
     blocks = {}
     for k, (_, dz, dy) in enumerate(order):
         blocks.setdefault((dz % Z, dy % Y), []).append(k)
@@ -424,7 +428,7 @@
             pltpu.VMEM((C * Y - 1, 2, 128), f32),
             pltpu.VMEM((Z, 2, 128), f32),
             pltpu.VMEM((X, Z, 2, 128), f32),
-            dma((5,)), dma((2,)), dma((1,)), dma((1,)), dma((1,)), dma((3,)), dma((3,)),
+            dma((5,)), dma((2,)), dma((1,)), dma((1,)), dma((1,)), dma((3,)), dma((4,)),
             dma((1,)), dma((1,)), dma((share_flags(plan()[0])[1],)), dma((2,)), dma((2,)),
             pltpu.SemaphoreType.REGULAR((2,)),
         ],

time: 71.1 us -> 70.8 us (level)
  no operation moved by 1% of the time
where the time goes in v7:
time: 70.8 us; the launch traced here: 70.7 us
  Pallas kernels  70.1 us (99%)
    pallas_call x1, Pallas kernels, local(): pl.pallas_call(gather_kernel, out_shape=(pltpu.VMEM((2, ROWS, COLS), bf16...  64.1 us
    pallas_call x1, Pallas kernels, local(): pl.pallas_call(write_kernel, out_shape=(jax.ShapeDtypeStruct((ROWS, COLS)...  5.96 us

profile of v7, /device:TPU:1, one launch (start us, length us, event | category | flops | bytes accessed | tf_op | source)
XLA Modules:
  0.0 70.7 jit_solution(3500780216705557291)
XLA Ops:
  0.6 64.1 %gather.1 = (bf16[2,2048,2048]{2,1,0:T(8,128)(2,1)S(1)}, f32[2,16,128]{2,1,0:T(8,128)S(1)}, f32[8,2,128]{2,1,0:T(2,128)S(1)}) custom-call(f32[32]{0:T(128)} %mix_h.1, f32[32,2048]{1,0:T(8,128)} %one_g.1, f32[32,2048]{1,0:T(8,128)} %other_g.1, f32[32,2048]{1,0:T(8,128)} %one_u.1, f32[32,2048]{1,0:T(8,128)} %other_u.1, f32[8]{0:T(128)} %train_h.1, f32[8]{0:T(128)} %step_h.1), custom_call_target="tpu_custom_call" | custom-call | tf_op jit(solution)/shard_map/gather/pallas_call | solution.py:407
  64.7 6.0 %write.1 = (bf16[2048,2048]{1,0:T(8,128)(2,1)}, bf16[2048,2048]{1,0:T(8,128)(2,1)}, f32[16,128]{1,0:T(8,128)}, f32[16,128]{1,0:T(8,128)}, bf16[16,128]{1,0:T(8,128)(2,1)}) custom-call(bf16[2,2048,2048]{2,1,0:T(8,128)(2,1)S(1)} %get-tuple-element.13.tiles, f32[2,16,128]{2,1,0:T(8,128)S(1)} %get-tuple-element.14.cols, f32[8,2,128]{2,1,0:T(2,128)S(1)} %get-tuple-element.15.norm), custom_call_target="tpu_custom_call" | custom-call | tf_op jit(solution)/shard_map/write/pallas_call | solution.py:446

commit v8 on v7

--- a/solution.py
+++ b/solution.py
@@ -18,9 +18,9 @@
 LOW = -3.0e38
 LATE = 24
 
-PIECES = (("A", 0, "own", 0, 6), ("B", 0, "own", 6, 16), ("A", 1, "other", 0, 7), ("B", 1, "other", 7, 16))
+PIECES = (("A", 1, "own", 0, 6), ("B", 0, "own", 6, 16), ("A", 0, "other", 0, 7), ("B", 1, "other", 7, 16))
 FIRST = (3, 1, 0, 2)
-EARLY = {"y": ((0, 2, 1), ()), "z": ((1,), (3,))}
+EARLY = {"y": ((0, 2, 3), ()), "z": ((1,), (3,))}
 LINKS = ("y+", "y-", "z+", "z-")
 STEP = {"y+": (0, 1), "y-": (0, -1), "z+": (1, 0), "z-": (-1, 0)}
 
@@ -51,8 +51,8 @@
     return (along_z if dy == 0 else []) + along_y
 
 
-def plan(hop=2.0, turn=0.04, block=5.6, swap=1.6, over_y=4.0, letters=0.9, over_z=8.5, work=0.08):
-    free = dict.fromkeys(LINKS, 0.0)
+def plan(hop=2.0, turn=0.04, block=5.6, swap=1.6, first=0.8, over_y=4.2, letters=0.9, over_z=8.2, work=0.08):
+    free = {link: first if link[0] == "y" else 0.0 for link in LINKS}
     queue, order, count = [], [], 0
 
     def put(piece, link, z, y, at, early=False):
@@ -374,7 +374,10 @@
     wide = [last - first for _, _, _, first, last in PIECES]
     soon = [sum(is_early(piece, link) for link in LINKS) for piece in range(len(PIECES))]
     arrived(out.at[0, pl.ds(0, 16 * sum(a * b for a, b in zip(soon, wide))), pl.ds(0, 512)], raw_send.at[0])
-    arrived(out.at[0, pl.ds(0, 2 * sum((Z * Y - 1 - a) * b for a, b in zip(soon, wide)))], send_sem.at[0])
+    tiles = OWN // 8 * sum((Z * Y - 1 - a) * b for a, b in zip(soon, wide))
+    across = max(w for w in range(1, TILES + 1) if tiles % w == 0)
+    deep = 1 if tiles // across <= ROWS // 8 else 2
+    arrived(out.at[pl.ds(0, deep), pl.ds(0, tiles // across // deep * 8), pl.ds(0, 128 * across)], send_sem.at[0])
     whole = out.at[0]
     arrived(whole, side_send.at[0])
     arrived(whole, side_recv.at[0])

time: 70.8 us -> 70.4 us (level)
  no operation moved by 1% of the time
where the time goes in v8:
time: 70.4 us; the launch traced here: 70.3 us
  Pallas kernels  69.6 us (99%)
    pallas_call x1, Pallas kernels, local(): pl.pallas_call(gather_kernel, out_shape=(pltpu.VMEM((2, ROWS, COLS), bf16...  63.7 us
    pallas_call x1, Pallas kernels, local(): pl.pallas_call(write_kernel, out_shape=(jax.ShapeDtypeStruct((ROWS, COLS)...  5.96 us

profile of v8, /device:TPU:1, one launch (start us, length us, event | category | flops | bytes accessed | tf_op | source)
XLA Modules:
  0.0 70.3 jit_solution(12335130593922287880)
XLA Ops:
  0.6 63.7 %gather.1 = (bf16[2,2048,2048]{2,1,0:T(8,128)(2,1)S(1)}, f32[2,16,128]{2,1,0:T(8,128)S(1)}, f32[8,2,128]{2,1,0:T(2,128)S(1)}) custom-call(f32[32]{0:T(128)} %mix_h.1, f32[32,2048]{1,0:T(8,128)} %one_g.1, f32[32,2048]{1,0:T(8,128)} %other_g.1, f32[32,2048]{1,0:T(8,128)} %one_u.1, f32[32,2048]{1,0:T(8,128)} %other_u.1, f32[8]{0:T(128)} %train_h.1, f32[8]{0:T(128)} %step_h.1), custom_call_target="tpu_custom_call" | custom-call | tf_op jit(solution)/shard_map/gather/pallas_call | solution.py:410
  64.3 6.0 %write.1 = (bf16[2048,2048]{1,0:T(8,128)(2,1)}, bf16[2048,2048]{1,0:T(8,128)(2,1)}, f32[16,128]{1,0:T(8,128)}, f32[16,128]{1,0:T(8,128)}, bf16[16,128]{1,0:T(8,128)(2,1)}) custom-call(bf16[2,2048,2048]{2,1,0:T(8,128)(2,1)S(1)} %get-tuple-element.13.tiles, f32[2,16,128]{2,1,0:T(8,128)S(1)} %get-tuple-element.14.cols, f32[8,2,128]{2,1,0:T(2,128)S(1)} %get-tuple-element.15.norm), custom_call_target="tpu_custom_call" | custom-call | tf_op jit(solution)/shard_map/write/pallas_call | solution.py:449

commit v9 on v8

--- a/solution.py
+++ b/solution.py
@@ -16,7 +16,7 @@
 CHIP = C * OWN
 TILES = COLS // 128
 LOW = -3.0e38
-LATE = 24
+LATE = 60
 
 PIECES = (("A", 1, "own", 0, 6), ("B", 0, "own", 6, 16), ("A", 0, "other", 0, 7), ("B", 1, "other", 7, 16))
 FIRST = (3, 1, 0, 2)
@@ -269,11 +269,11 @@
     for d in range(C * Y - 1):
         line = jnp.maximum(line, row_yc[d])
     rows_z[z] = line
-    for d in range(1, Z):
-        remote(rows_z.at[z], rows_z.at[z], norm_send.at[1], norm_sem.at[1], z_at[d]).start()
     for link in LINKS:
         for piece in EARLY[link[0]][1]:
             early(piece, link).start()
+    for d in range(1, Z):
+        remote(rows_z.at[z], rows_z.at[z], norm_send.at[1], norm_sem.at[1], z_at[d]).start()
     arrived(peak_z.at[pl.ds(1, Z - 1)], z_sem.at[0])
     for d in range(1, Z):
         best = jnp.maximum(best, peak_z[d])
@@ -327,11 +327,13 @@
         for piece in range(len(PIECES)):
             if (piece, 0, 0) not in order:
                 scale(piece, x, home)
+
+    def own_aside():
         send_aside(home)
         remote(cols.at[c], cols.at[c], side_send.at[1], side_recv.at[1], sibling).start()
 
     n = len(order)
-    aside = {n // 8: own_rest, n // 4: norm_beside, n // 2: norm_across, 3 * n // 4: norm_done}
+    aside = {n // 8: own_rest, n // 8 + 2: own_aside, n // 4: norm_beside, n // 2: norm_across, 3 * n // 4: norm_done}
     blocks = {}
     for k, (_, dz, dy) in enumerate(order):
         blocks.setdefault((dz % Z, dy % Y), []).append(k)
@@ -377,6 +379,7 @@
     tiles = OWN // 8 * sum((Z * Y - 1 - a) * b for a, b in zip(soon, wide))
     across = max(w for w in range(1, TILES + 1) if tiles % w == 0)
     deep = 1 if tiles // across <= ROWS // 8 else 2
+    assert tiles % (across * deep) == 0
     arrived(out.at[pl.ds(0, deep), pl.ds(0, tiles // across // deep * 8), pl.ds(0, 128 * across)], send_sem.at[0])
     whole = out.at[0]
     arrived(whole, side_send.at[0])

time: 70.4 us -> 70.4 us (level)
  no operation moved by 1% of the time
where the time goes in v9:
time: 70.4 us; the launch traced here: 70.3 us
  Pallas kernels  69.6 us (99%)
    pallas_call x1, Pallas kernels, local(): pl.pallas_call(gather_kernel, out_shape=(pltpu.VMEM((2, ROWS, COLS), bf16...  63.7 us
    pallas_call x1, Pallas kernels, local(): pl.pallas_call(write_kernel, out_shape=(jax.ShapeDtypeStruct((ROWS, COLS)...  5.96 us

profile of v9, /device:TPU:1, one launch (start us, length us, event | category | flops | bytes accessed | tf_op | source)
XLA Modules:
  0.0 70.3 jit_solution(1886839957831998883)
XLA Ops:
  0.6 63.7 %gather.1 = (bf16[2,2048,2048]{2,1,0:T(8,128)(2,1)S(1)}, f32[2,16,128]{2,1,0:T(8,128)S(1)}, f32[8,2,128]{2,1,0:T(2,128)S(1)}) custom-call(f32[32]{0:T(128)} %mix_h.1, f32[32,2048]{1,0:T(8,128)} %one_g.1, f32[32,2048]{1,0:T(8,128)} %other_g.1, f32[32,2048]{1,0:T(8,128)} %one_u.1, f32[32,2048]{1,0:T(8,128)} %other_u.1, f32[8]{0:T(128)} %train_h.1, f32[8]{0:T(128)} %step_h.1), custom_call_target="tpu_custom_call" | custom-call | tf_op jit(solution)/shard_map/gather/pallas_call | solution.py:413
  64.3 6.0 %write.1 = (bf16[2048,2048]{1,0:T(8,128)(2,1)}, bf16[2048,2048]{1,0:T(8,128)(2,1)}, f32[16,128]{1,0:T(8,128)}, f32[16,128]{1,0:T(8,128)}, bf16[16,128]{1,0:T(8,128)(2,1)}) custom-call(bf16[2,2048,2048]{2,1,0:T(8,128)(2,1)S(1)} %get-tuple-element.13.tiles, f32[2,16,128]{2,1,0:T(8,128)S(1)} %get-tuple-element.14.cols, f32[8,2,128]{2,1,0:T(2,128)S(1)} %get-tuple-element.15.norm), custom_call_target="tpu_custom_call" | custom-call | tf_op jit(solution)/shard_map/write/pallas_call | solution.py:452

commit v10 on v9

--- a/solution.py
+++ b/solution.py
@@ -105,13 +105,21 @@
             if before[1:] != (0, 0) or not is_early(event[0], link):
                 back = link[0] + ("-" if link[1] == "+" else "+")
                 known[back][k] = max(known[back][k], at[before])
-    flags, last = {}, []
+    flags, last, twins = {}, [], {}
     for k, event in enumerate(order):
-        if event[1:] == (0, 0):
+        if event[1:] == (0, 0) or event in flags:
             continue
         link, before = came_by(*event)
         early = before[1:] == (0, 0) and is_early(event[0], link)
-        free = [] if early else [i for i, used in enumerate(last) if used <= known[link][at[before]]]
+        seen = -1 if early else known[link][at[before]]
+        twin = order[k + 1] if k + 1 < len(order) else None
+        if twin in ((event[0], -event[1], event[2]), (event[0], event[1], -event[2])):
+            link2, before2 = came_by(*twin)
+            if (before2[1:] == (0, 0) and is_early(twin[0], link2)) == early:
+                twins[event] = twin
+                if not early:
+                    seen = min(seen, known[link2][at[before2]])
+        free = [] if early else [i for i, used in enumerate(last) if used <= seen]
         if free:
             i = min(free, key=lambda i: last[i])
             last[i] = k
@@ -119,7 +127,9 @@
             i = len(last)
             last.append(k)
         flags[event] = i
-    return flags, len(last)
+        if event in twins:
+            flags[twins[event]] = i
+    return flags, len(last), twins
 
 
 def gather_kernel(
@@ -131,7 +141,8 @@
     raw_send, send_sem, recv_sem, side_send, side_recv, known,
 ):
     order, _ = plan()
-    flags, _ = share_flags(order)
+    flags, _, twins = share_flags(order)
+    waited = set(twins.values())
     z, y, c, m = (lax.axis_index(a) for a in SHARD_MODEL)
     mesh_id = pl.DeviceIdType.MESH
     z_at = [(lax.rem(z + d, Z), y, c, m) for d in range(Z)]
@@ -348,11 +359,14 @@
         if (dz, dy) == (0, 0):
             scale(piece, x, base)
         elif computed:
-            early(piece, link).wait_recv()
+            if (piece, dz, dy) not in waited:
+                pair = 2 if (piece, dz, dy) in twins else 1
+                arrived(ins.at[pl.ds(0, pair), :, lanes_of(piece)], flag(piece, dz, dy))
             scale(piece, raw.at[LINKS.index(link)], base)
         else:
-            ref = out.at[c, pl.ds(pl.multiple_of(base + rows_of(piece), OWN), OWN), lanes_of(piece)]
-            remote(ref, ref, send_sem.at[0], flag(piece, dz, dy), sibling).wait_recv()
+            if (piece, dz, dy) not in waited:
+                pair = 2 if (piece, dz, dy) in twins else 1
+                arrived(out.at[0, pl.ds(0, pair * OWN), lanes_of(piece)], flag(piece, dz, dy))
         if pending:
             send_on(*pending)
         pending = (piece, dz, dy, base)

time: 70.4 us -> 70.3 us (level)
  no operation moved by 1% of the time
where the time goes in v10:
time: 70.3 us; the launch traced here: 70.2 us
  Pallas kernels  69.5 us (99%)
    pallas_call x1, Pallas kernels, local(): pl.pallas_call(gather_kernel, out_shape=(pltpu.VMEM((2, ROWS, COLS), bf16...  63.6 us
    pallas_call x1, Pallas kernels, local(): pl.pallas_call(write_kernel, out_shape=(jax.ShapeDtypeStruct((ROWS, COLS)...  5.96 us

profile of v10, /device:TPU:1, one launch (start us, length us, event | category | flops | bytes accessed | tf_op | source)
XLA Modules:
  0.0 70.2 jit_solution(14164768463996903685)
XLA Ops:
  0.6 63.6 %gather.1 = (bf16[2,2048,2048]{2,1,0:T(8,128)(2,1)S(1)}, f32[2,16,128]{2,1,0:T(8,128)S(1)}, f32[8,2,128]{2,1,0:T(2,128)S(1)}) custom-call(f32[32]{0:T(128)} %mix_h.1, f32[32,2048]{1,0:T(8,128)} %one_g.1, f32[32,2048]{1,0:T(8,128)} %other_g.1, f32[32,2048]{1,0:T(8,128)} %one_u.1, f32[32,2048]{1,0:T(8,128)} %other_u.1, f32[8]{0:T(128)} %train_h.1, f32[8]{0:T(128)} %step_h.1), custom_call_target="tpu_custom_call" | custom-call | tf_op jit(solution)/shard_map/gather/pallas_call | solution.py:427
  64.2 6.0 %write.1 = (bf16[2048,2048]{1,0:T(8,128)(2,1)}, bf16[2048,2048]{1,0:T(8,128)(2,1)}, f32[16,128]{1,0:T(8,128)}, f32[16,128]{1,0:T(8,128)}, bf16[16,128]{1,0:T(8,128)(2,1)}) custom-call(bf16[2,2048,2048]{2,1,0:T(8,128)(2,1)S(1)} %get-tuple-element.13.tiles, f32[2,16,128]{2,1,0:T(8,128)S(1)} %get-tuple-element.14.cols, f32[8,2,128]{2,1,0:T(2,128)S(1)} %get-tuple-element.15.norm), custom_call_target="tpu_custom_call" | custom-call | tf_op jit(solution)/shard_map/write/pallas_call | solution.py:466

commit v11 on v10

--- a/solution.py
+++ b/solution.py
@@ -20,7 +20,7 @@
 
 PIECES = (("A", 1, "own", 0, 6), ("B", 0, "own", 6, 16), ("A", 0, "other", 0, 7), ("B", 1, "other", 7, 16))
 FIRST = (3, 1, 0, 2)
-EARLY = {"y": ((0, 2, 3), ()), "z": ((1,), (3,))}
+EARLY = {"y": ((0, 2, 1), ()), "z": ((1,), (3,))}
 LINKS = ("y+", "y-", "z+", "z-")
 STEP = {"y+": (0, 1), "y-": (0, -1), "z+": (1, 0), "z-": (-1, 0)}
 

time: 70.3 us -> 70.4 us (level)
  no operation moved by 1% of the time
where the time goes in v11:
time: 70.4 us; the launch traced here: 70.3 us
  Pallas kernels  69.6 us (99%)
    pallas_call x1, Pallas kernels, local(): pl.pallas_call(gather_kernel, out_shape=(pltpu.VMEM((2, ROWS, COLS), bf16...  63.7 us
    pallas_call x1, Pallas kernels, local(): pl.pallas_call(write_kernel, out_shape=(jax.ShapeDtypeStruct((ROWS, COLS)...  5.96 us

profile of v11, /device:TPU:1, one launch (start us, length us, event | category | flops | bytes accessed | tf_op | source)
XLA Modules:
  0.0 70.3 jit_solution(7557182353512656605)
XLA Ops:
  0.6 63.7 %gather.1 = (bf16[2,2048,2048]{2,1,0:T(8,128)(2,1)S(1)}, f32[2,16,128]{2,1,0:T(8,128)S(1)}, f32[8,2,128]{2,1,0:T(2,128)S(1)}) custom-call(f32[32]{0:T(128)} %mix_h.1, f32[32,2048]{1,0:T(8,128)} %one_g.1, f32[32,2048]{1,0:T(8,128)} %other_g.1, f32[32,2048]{1,0:T(8,128)} %one_u.1, f32[32,2048]{1,0:T(8,128)} %other_u.1, f32[8]{0:T(128)} %train_h.1, f32[8]{0:T(128)} %step_h.1), custom_call_target="tpu_custom_call" | custom-call | tf_op jit(solution)/shard_map/gather/pallas_call | solution.py:427
  64.3 6.0 %write.1 = (bf16[2048,2048]{1,0:T(8,128)(2,1)}, bf16[2048,2048]{1,0:T(8,128)(2,1)}, f32[16,128]{1,0:T(8,128)}, f32[16,128]{1,0:T(8,128)}, bf16[16,128]{1,0:T(8,128)(2,1)}) custom-call(bf16[2,2048,2048]{2,1,0:T(8,128)(2,1)S(1)} %get-tuple-element.13.tiles, f32[2,16,128]{2,1,0:T(8,128)S(1)} %get-tuple-element.14.cols, f32[8,2,128]{2,1,0:T(2,128)S(1)} %get-tuple-element.15.norm), custom_call_target="tpu_custom_call" | custom-call | tf_op jit(solution)/shard_map/write/pallas_call | solution.py:466
